TPU v7x, 512 devices: a whole 4x4x16 slice. The times are simulated.
512 devices in a mesh: row: 16 (over z), col: 32 (over x, y, core).
Axes of the slice: x: 4, y: 4, z: 16, core: 2. Of those that a mesh axis runs over, the one named last changes fastest.
Arguments:
- train_points: float32 [16, 32, 16384], P('row', None, 'col'), as said below
- targets: float32 [16, 16384], P('row', 'col'), may hold values from -16 to 16
- inverse_factor: float32 [16, 16384, 1024], P('row', 'col')
- counts: int32 [16, 16], P('row'), may hold values from 512 to 1024, as said below
- membership: int32 [16, 16, 64], replicated, may hold values from 0 to 1, as said below
- test_points: float32 [64, 32, 128], P('row'), may hold values from -6 to 6
Outputs:
- pred_mean: float32 [64, 128], P('row')
- pred_var: float32 [64, 128], P('row')
Inputs may be any that keep to these rules, and one draw needn't show every extreme that they name: Each expert membership[r, c, :] takes part in at least one and at most 8 blocks, exactly 8 for at least one expert, and in at most one of the 4 blocks of each owner row. `counts`: at least one expert has all 1024 points valid. `train_points`: each expert's 1024 points are drawn independently of the other experts' points.
All inputs are finite; a program needn't handle non-finite values.
Results may differ from a plain program's by a relative error of at most 0.0003.
Values sent between devices are 32-bit elements; how exact they have to be, the bound alone decides.
No kernel may reach another device: no remote copies, remote signals or barrier semaphores. Data moves between devices by JAX's collectives and lax.ppermute only.
A program may use at most 64 MiB of HBM per device.

v0:
```python
import jax
import jax.numpy as jnp
from jax import lax
from jax.sharding import PartitionSpec as P

SIGNAL = 1.0
NOISE = 0.1
HIGHEST = lax.Precision.HIGHEST


def partner_2(block, axis, distance):
    count = lax.axis_size(axis)
    route = []
    for low in range(count):
        high = low | 1 << distance
        if high != low and high < count:
            route += [(low, high), (high, low)]
    return lax.ppermute(block, axis, route)


def in_blocks(x, dim, peers):
    before, after = (x.shape[:dim], x.shape[dim + 1 :])
    return jnp.moveaxis(x.reshape(*before, peers, -1, *after), dim, 0)


def sent_and_summed(x, axis, dim):
    parts = in_blocks(x, dim, lax.axis_size(axis))
    arrived = lax.all_to_all(parts, axis, split_axis=0, concat_axis=0, tiled=True)
    return arrived.sum(axis=0)


def side_by_side(arrays, axis, dim, along):
    ends, at = ([], 0)
    for a in arrays[:-1]:
        at += a.shape[along]
        ends.append(at)
    both = jnp.concatenate(arrays, axis=along)
    return tuple(jnp.split(sent_and_summed(both, axis, dim), ends, axis=along))


def sent_to_all(x, axis):
    peers = lax.axis_size(axis)
    return lax.all_to_all(jnp.broadcast_to(x[None], (peers, *x.shape)), axis, 0, 0, tiled=True)


def of_everyone(x, axis):
    return sent_to_all(x, axis).sum(axis=0)


def together(arrays, axis):
    ravelled, at, done = (jnp.concatenate([a.reshape(-1) for a in arrays]), 0, [])
    total = of_everyone(ravelled, axis)
    for a in arrays:
        done.append(total[at : at + a.size].reshape(a.shape))
        at += a.size
    return tuple(done)


def cross_kernel(train_cols, test_cols, squared_scale):
    products = jnp.einsum("dn,dp->np", train_cols, test_cols, precision=HIGHEST)
    spread = (
        jnp.sum(train_cols * train_cols, axis=0)[:, None]
        + jnp.sum(test_cols * test_cols, axis=0)[None, :]
        - 2.0 * products
    )
    return SIGNAL * jnp.exp(-0.5 * spread / squared_scale)


def slot_table(member, slot_count):
    before = jnp.cumsum(member) - member
    slot_ids = jnp.arange(slot_count, dtype=jnp.int32)[:, None]
    picked = ((member[None, :] == 1) & (before[None, :] == slot_ids)).astype(jnp.int32)
    chosen = jnp.sum(picked * jnp.arange(member.shape[0], dtype=jnp.int32)[None, :], axis=1)
    return (picked.astype(jnp.float32), chosen)


def weigh_expert(mean_part, quad_part):
    variance = NOISE + jnp.maximum(SIGNAL - quad_part, 0.0)
    entropy_gap = 0.5 * (jnp.log(SIGNAL + NOISE) - jnp.log(variance))
    weight = entropy_gap / variance
    return (weight * mean_part, weight)


def on_device(train_points, targets, inverse_factor, counts, membership, test_points):
    parity = lax.axis_index("col") % 2
    expert_col = lax.axis_index("col") // 2
    own_row = lax.axis_index("row")
    row_count = lax.axis_size("row")
    slot_count = min(8, row_count)
    features = train_points.shape[1]
    rows_half = train_points.shape[2]
    blocks_own = test_points.shape[0]
    block_len = test_points.shape[2]
    squared_scale = 0.5 * features
    own_points = train_points[0]
    own_targets = targets[0]
    packed = jnp.concatenate([own_points, own_targets[None, :]], axis=0)
    partner = partner_2(packed, "col", 0)
    other_points = partner[:features]
    other_targets = partner[features]
    member = membership[own_row, expert_col]
    picked, chosen = slot_table(member, slot_count)
    wanted = lax.dynamic_slice_in_dim(
        membership[:, expert_col], own_row * blocks_own, blocks_own, 1
    )
    outgoing = jnp.einsum("rj,jdb->rdb", wanted.astype(jnp.float32), test_points, precision=HIGHEST)
    incoming = lax.all_to_all(outgoing, "row", split_axis=0, concat_axis=0, tiled=True)
    slot_tests = incoming[chosen // blocks_own]
    test_cols = slot_tests.transpose(1, 0, 2).reshape(features, slot_count * block_len)
    valid_count = counts[0, expert_col]
    local_index = jnp.arange(rows_half, dtype=jnp.int32)
    own_valid = 2 * local_index + parity < valid_count
    other_valid = 2 * local_index + (1 - parity) < valid_count
    own_kernel = jnp.where(
        own_valid[:, None], cross_kernel(own_points, test_cols, squared_scale), 0.0
    )
    other_kernel = jnp.where(
        other_valid[:, None], cross_kernel(other_points, test_cols, squared_scale), 0.0
    )
    factor_pairs = inverse_factor[0].reshape(rows_half, rows_half, 2)
    own_part = lax.dynamic_index_in_dim(factor_pairs, parity, 2, keepdims=False)
    other_part = lax.dynamic_index_in_dim(factor_pairs, 1 - parity, 2, keepdims=False)
    solved = jnp.dot(own_part, own_kernel, precision=HIGHEST, preferred_element_type=jnp.float32)
    solved = solved + jnp.dot(
        other_part, other_kernel, precision=HIGHEST, preferred_element_type=jnp.float32
    )
    whitened = jnp.dot(own_part, own_targets, precision=HIGHEST, preferred_element_type=jnp.float32)
    whitened = whitened + jnp.dot(
        other_part, other_targets, precision=HIGHEST, preferred_element_type=jnp.float32
    )
    mean_own = jnp.dot(whitened, solved, precision=HIGHEST, preferred_element_type=jnp.float32)
    quad_own = jnp.sum(solved * solved, axis=0)
    partials = partner_2(jnp.stack([mean_own, quad_own], axis=0), "col", 0)
    weighted, weight = weigh_expert(mean_own + partials[0], quad_own + partials[1])
    slot_ids = jnp.arange(slot_count, dtype=jnp.int32)
    my_slots = (slot_ids % 2 == parity).astype(jnp.float32)[:, None]
    my_picked = picked * my_slots
    dense_num = jnp.einsum(
        "sb,sp->bp", my_picked, weighted.reshape(slot_count, block_len), precision=HIGHEST
    )
    dense_wgt = jnp.einsum(
        "sb,sp->bp", my_picked, weight.reshape(slot_count, block_len), precision=HIGHEST
    )
    share_num, share_wgt = side_by_side((dense_num, dense_wgt), "row", 0, 1)
    total_num, total_wgt = together((share_num, share_wgt), "col")
    precision_sum = 1.0 / (SIGNAL + NOISE) + total_wgt
    return (total_num / precision_sum, 1.0 / precision_sum)


def solution(mesh):
    in_specs = (
        P("row", None, "col"),
        P("row", "col"),
        P("row", "col", None),
        P("row", None),
        P(),
        P("row", None, None),
    )
    out_specs = (P("row", None), P("row", None))
    return jax.shard_map(
        on_device, mesh=mesh, in_specs=in_specs, out_specs=out_specs, check_vma=False
    )
```

profile of v0, /device:TPU:1, one launch (start us, length us, event | category | flops | bytes accessed | tf_op | source)
XLA Modules:
  0.0 100.9 jit_solution(7095147673971829736)
XLA Ops:
  0.6 0.0 copy-start
  0.7 0.9 constant_dynamic-slice_fusion.1
  1.6 0.1 copy.67
  1.7 0.0 copy-done
  1.7 0.5 fusion.42
  2.2 0.8 copy.60
  3.0 15.7 %all-to-all-start = ((f32[16,32,128]{2,1,0:T(8,128)}), f32[16,32,128]{2,1,0:T(8,128)S(1)}, u32[]{:S(2)}, u32[]{:S(2)}) async-start(f32[16,32,128]{2,1,0:T(8,128)} %copy.60), calls=%async_computation | async-start | bytes 524288 | tf_op jit(solution)/shard_map/all_to_all | solution.py:107
  18.7 1.5 %pad_maximum_fusion = f32[33,512]{1,0:T(8,128)} fusion(f32[1,512]{1,0:T(1,128)} %param.7, f32[32,512]{1,0:T(8,128)} %bitcast.105), kind=kLoop, calls=%fused_computation.43 | loop fusion | flops 16896 | bytes 135168 | tf_op jit(solution)/shard_map/concatenate | solution.py:97
  20.2 2.9 %collective-permute-start = (f32[33,512]{1,0:T(8,128)}, f32[33,512]{1,0:T(8,128)}, u32[]{:S(2)}, u32[]{:S(2)}) collective-permute-start(f32[33,512]{1,0:T(8,128)} %pad_maximum_fusion), channel_id=1, source_target_pairs={{0,1},{1,0},{2,3},{3,2},{4,5},{5,4},{6,7},{7,6},{8,9},{9,8},{10,11... | collective-permute-start | bytes 202760 | tf_op jit(solution)/shard_map/ppermute | solution.py:18
  23.1 3.0 %copy.56 = f32[1,512,1024]{1,2,0:T(8,128)} copy(f32[1,512,1024]{2,1,0:T(8,128)} %param.8) | data formatting | bytes 4194304 | tf_op args[2]
  26.0 0.0 copy-start.3
  26.0 2.5 %reshape_squeeze.3 = f32[512,512,2]{0,2,1:T(2,128)S(1)} reshape(f32[1,512,1024]{1,2,0:T(8,128)} %copy.56) | data formatting | bytes 4194304 | tf_op jit(solution)/shard_map/reshape;squeeze | solution.py:120
  28.5 0.7 bitcast_compare_fusion
  29.2 0.1 copy.55
  29.3 0.1 reduce-window.8
  29.4 0.1 reduce.2
  29.6 0.0 copy-start.4
  29.6 0.1 select_reduce_fusion
  29.7 0.0 copy-done.3
  29.7 0.6 constant_dynamic-slice_fusion.2
  30.3 2.8 %constant_dynamic-slice_fusion = (f32[512,512,1]{0,2,1:T(1,128)S(1)}, f32[512,512,1]{0,2,1:T(1,128)}) fusion(f32[512,512,2]{0,2,1:T(2,128)S(1)} %reshape_squeeze.3, s32[]{:T(128)S(6)} %select_n.84, s32[]{:T(128)S(6)} %select_n.77), kind=kLoop, calls=%fused_computation.111 | loop fusion | bytes 4194312 | tf_op jit(solution)/shard_map/jit(dynamic_index_in_dim)/dynamic_slice | solution.py:122
  33.1 0.0 copy-done.4
  33.1 0.7 add_compare_fusion.1
  33.7 0.0 copy-start.1
  33.8 0.0 copy-start.2
  33.8 2.4 %copy.57 = f32[512,512,1]{1,0,2:T(8,128)S(1)} copy(f32[512,512,1]{0,2,1:T(1,128)} %get-tuple-element.5) | data formatting | bytes 2097152 | tf_op jit(solution)/shard_map/jit(dynamic_index_in_dim)/dynamic_slice | solution.py:121
  36.2 1.5 %copy.62 = f32[512,512,1]{1,0,2:T(8,128)S(1)} copy(f32[512,512,1]{0,2,1:T(1,128)S(1)} %get-tuple-element.4) | data formatting | bytes 2097152 | tf_op jit(solution)/shard_map/jit(dynamic_index_in_dim)/dynamic_slice | solution.py:122
  37.7 0.0 copy-done.1
  37.7 0.0 copy-done.2
  37.7 1.0 fusion.20
  38.7 0.7 add_compare_fusion
  39.4 0.0 collective-permute-done
  39.4 1.7 %fusion.17 = f32[1,512]{1,0:T(1,128)S(1)} fusion(f32[512,512,1]{1,0,2:T(8,128)S(1)} %copy.62, f32[33,512]{1,0:T(8,128)} %collective-permute-done), kind=kOutput, calls=%fused_computation.17 | convolution fusion | flops 3145728 | bytes 1052672 | tf_op jit(solution)/shard_map/dot_general | solution.py:128
  41.1 0.9 multiply_reduce_fusion.1
  42.0 0.0 all-to-all-done
  42.0 0.6 gather_fusion
  42.5 1.8 %fusion.37 = f32[1024,512]{1,0:T(8,128)S(1)} fusion(f32[1,32,512]{2,1,0:T(8,128)S(1)} %copy-done.1, f32[8,32,128]{2,1,0:T(8,128)S(1)} %gather_fusion), kind=kOutput, calls=%fused_computation.37 | convolution fusion | flops 201326592 | bytes 2293760 | tf_op jit(solution)/shard_map/dn,dp->np/dot_general | solution.py:60
  44.4 4.1 %fusion.3 = f32[512,1024]{1,0:T(8,128)S(1)} fusion(f32[1024,512]{1,0:T(8,128)S(1)} %fusion.37, f32[512,512,1]{1,0,2:T(8,128)S(1)} %copy.57, f32[1024]{0:T(1024)S(1)} %bitcast.106, f32[512]{0:T(512)S(1)} %multiply_reduce_fusion.2, pred[512]{0:T(512)(128)(4,1)S(1)} %add_compare_fusion.1), kind=kOutput, calls=%fused_computation.5 | convolution fusion | flops 3223846912 | bytes 5249536 | tf_op jit(solution)/shard_map/dot_general | solution.py:123
  48.5 2.7 %fusion.35 = f32[512,1024]{0,1:T(8,128)S(1)} fusion(f32[33,512]{1,0:T(8,128)} %collective-permute-done, f32[8,32,128]{2,1,0:T(8,128)S(1)} %gather_fusion), kind=kOutput, calls=%fused_computation.35 | convolution fusion | flops 201326592 | bytes 2293760 | tf_op jit(solution)/shard_map/dn,dp->np/dot_general | solution.py:60
  51.2 4.2 %multiply_reduce_fusion = (f32[1024]{0:T(1024)S(1)}, f32[512,1024]{1,0:T(8,128)S(1)}) fusion(f32[512,1024]{1,0:T(8,128)S(1)} %fusion.3, f32[512,1024]{0,1:T(8,128)S(1)} %fusion.35, f32[512]{0:T(512)S(1)} %multiply_reduce_fusion.1, f32[1024]{0:T(1024)S(1)} %bitcast.107, pred[512]{0:T(512)(128)(4,1)S(1)} %add_compare_fusion, f32[512,512,1]{1,0,2:T(8,128)S(1)} %copy.62), kind=kOutput, calls=%fused_computation.6 | convolution fusion | flops 3225418752 | bytes 7350784 | tf_op jit(solution)/shard_map/dot_general | solution.py:124
  55.3 0.0 copy-start.5
  55.4 1.1 %fusion.108 = f32[1,1024]{1,0:T(1,128)S(1)} fusion(f32[512,1]{0,1:T(1,128)S(1)} %bitcast.110, f32[512,1024]{1,0:T(8,128)S(1)} %get-tuple-element.13), kind=kOutput, calls=%fused_computation.141 | convolution fusion | flops 6291456 | bytes 2103296 | tf_op jit(solution)/shard_map/dot_general | solution.py:131
  56.5 1.9 %collective-permute-start.1 = (f32[2,1024]{1,0:T(2,128)S(1)}, f32[2,1024]{1,0:T(2,128)S(1)}, u32[]{:S(2)}, u32[]{:S(2)}) collective-permute-start(f32[2,1024]{1,0:T(2,128)S(1)} %pad_maximum_fusion.2), channel_id=1, source_target_pairs={{0,1},{1,0},{2,3},{3,2},{4,5},{5,4},{6,7},{7,6},{8,9},{9,8},{10,11... | collective-permute-start | bytes 24584 | tf_op jit(solution)/shard_map/ppermute | solution.py:18
  58.4 1.1 %collective-permute-done.1 = f32[2,1024]{1,0:T(2,128)S(1)} collective-permute-done((f32[2,1024]{1,0:T(2,128)S(1)}, f32[2,1024]{1,0:T(2,128)S(1)}, u32[]{:S(2)}, u32[]{:S(2)}) %collective-permute-start.1) | collective-permute-done | bytes 8224 | tf_op jit(solution)/shard_map/ppermute | solution.py:18
  59.5 0.0 copy-done.5
  59.6 0.3 fusion.50
  59.9 0.3 fusion.48
  60.2 23.1 %all_to_all.16 = f32[16,4,256]{2,1,0:T(4,128)S(1)} all-to-all(f32[16,4,256]{2,1,0:T(4,128)S(1)} %reshape.180), channel_id=1, replica_groups=mesh['row'=16,'col'=32] {'row'}, dimensions={0} | all-to-all | bytes 131072 | tf_op jit(solution)/shard_map/all_to_all | solution.py:28
  83.4 0.1 broadcast_in_dim.38
  83.5 16.7 %all_to_all.17 = f32[32,1,1024]{2,1,0:T(1,128)S(1)} all-to-all(f32[32,1,1024]{2,1,0:T(1,128)S(1)} %broadcast_in_dim.38), channel_id=1, replica_groups=mesh['row'=16,'col'=32] {'col'}, dimensions={0} | all-to-all | bytes 262144 | tf_op jit(solution)/shard_map/all_to_all | solution.py:43
  100.2 0.1 reduce_sum.79
  100.3 0.6 divide_bitcast_fusion
  (14 shorter events, 0.2 us)
Async XLA Ops:
  0.6 1.1 %copy-start = (f32[4,32,128]{2,1,0:T(8,128)S(1)}, f32[4,32,128]{2,1,0:T(8,128)}, u32[]{:S(2)}) copy-start(f32[4,32,128]{2,1,0:T(8,128)} %param.11) | copy-start | bytes 196612
  3.0 39.0 %all-to-all-start = ((f32[16,32,128]{2,1,0:T(8,128)}), f32[16,32,128]{2,1,0:T(8,128)S(1)}, u32[]{:S(2)}, u32[]{:S(2)}) async-start(f32[16,32,128]{2,1,0:T(8,128)} %copy.60), calls=%async_computation | async-start | bytes 524288 | tf_op jit(solution)/shard_map/all_to_all | solution.py:107
  20.2 19.2 %collective-permute-start = (f32[33,512]{1,0:T(8,128)}, f32[33,512]{1,0:T(8,128)}, u32[]{:S(2)}, u32[]{:S(2)}) collective-permute-start(f32[33,512]{1,0:T(8,128)} %pad_maximum_fusion), channel_id=1, source_target_pairs={{0,1},{1,0},{2,3},{3,2},{4,5},{5,4},{6,7},{7,6},{8,9},{9,8},{10,11... | collective-permute-start | bytes 202760 | tf_op jit(solution)/shard_map/ppermute | solution.py:18
  26.0 3.7 %copy-start.3 = (s32[1,16]{1,0:T(1,128)S(1)}, s32[1,16]{1,0:T(1,128)}, u32[]{:S(2)}) copy-start(s32[1,16]{1,0:T(1,128)} %param.9) | copy-start | bytes 196
  29.6 3.5 %copy-start.4 = (s32[64]{0:T(128)}, s32[64]{0:T(128)S(1)}, u32[]{:S(2)}) copy-start(s32[64]{0:T(128)S(1)} %bitcast_subtract_fusion.1) | copy-start | bytes 772
  33.7 3.9 %copy-start.1 = (f32[1,32,512]{2,1,0:T(8,128)S(1)}, f32[1,32,512]{2,1,0:T(8,128)}, u32[]{:S(2)}) copy-start(f32[1,32,512]{2,1,0:T(8,128)} %param.6) | copy-start | bytes 196612
  33.8 3.9 %copy-start.2 = (f32[1,512]{1,0:T(1,128)S(1)}, f32[1,512]{1,0:T(1,128)}, u32[]{:S(2)}) copy-start(f32[1,512]{1,0:T(1,128)} %param.7) | copy-start | bytes 6148
  55.3 4.2 %copy-start.5 = (s32[64]{0:T(128)S(1)}, s32[64]{0:T(128)}, u32[]{:S(2)}) copy-start(s32[64]{0:T(128)} %copy-done.4) | copy-start | bytes 772
  56.5 3.1 %collective-permute-start.1 = (f32[2,1024]{1,0:T(2,128)S(1)}, f32[2,1024]{1,0:T(2,128)S(1)}, u32[]{:S(2)}, u32[]{:S(2)}) collective-permute-start(f32[2,1024]{1,0:T(2,128)S(1)} %pad_maximum_fusion.2), channel_id=1, source_target_pairs={{0,1},{1,0},{2,3},{3,2},{4,5},{5,4},{6,7},{7,6},{8,9},{9,8},{10,11... | collective-permute-start | bytes 24584 | tf_op jit(solution)/shard_map/ppermute | solution.py:18
where the time goes:
time: 102 us; the launch traced here: 101 us
  blocking collectives  39.8 us (39%)
  starting transfers between devices  20.5 us (20%)
  matrix products  17.6 us (17%)
  local copies, waits for them, and re-layouts  15.3 us (15%)
  other arithmetic  5.55 us (5%)
  waiting for transfers between devices  1.13 us (1%)
    all_to_all x1, blocking collectives, sent_and_summed(): lax.all_to_all(parts, axis, split_axis=0, concat_axis=0, tiled=True)  23.1 us
    all_to_all x1, blocking collectives, sent_to_all(): lax.all_to_all(jnp.broadcast_to(x[None], (peers, *x.shape)), axis, 0, 0,...  16.7 us
    all_to_all x1, starting transfers between devices, on_device(): lax.all_to_all(outgoing, 'row', split_axis=0, concat_axis=0, tiled=True)  15.7 us
    ppermute x2, starting transfers between devices, partner_2(): return lax.ppermute(block, axis, route)  4.77 us
    dot_general x2, matrix products, cross_kernel(): products = jnp.einsum('dn,dp->np', train_cols, test_cols, precision=HIGHEST)  4.52 us
    dynamic_slice x2, local copies, waits for them, and re-layouts, on_device(): lax.dynamic_index_in_dim(factor_pairs, 1 - parity, 2, keepdims=False)  4.28 us
    dot_general x1, matrix products, on_device(): jnp.dot(other_part, other_kernel, precision=HIGHEST, preferred_element_ty...  4.17 us
    dot_general x1, matrix products, on_device(): jnp.dot(own_part, own_kernel, precision=HIGHEST, preferred_element_type=j...  4.05 us
  transfers between devices with their start and end apart: 3, of which 1 were waited for; matrix products, arithmetic and copies ran while one was open for 20% of the time, Pallas kernels for 0%

commit v1 on v0

v1 whole, which is shorter than its diff:
```python
import math

import jax
import jax.numpy as jnp
from jax import lax
from jax.experimental import pallas as pl
from jax.experimental.pallas import tpu as pltpu
from jax.sharding import PartitionSpec as P

SIGNAL = 1.0
NOISE = 0.1
BF16 = jnp.bfloat16
F32 = jnp.float32
I32 = jnp.int32
LANES = 128
SUBLANES = 8


def three_parts(v):
    high = v.astype(BF16).astype(F32)
    rest = v - high
    mid = rest.astype(BF16).astype(F32)
    return high, mid, (rest - mid).astype(BF16).astype(F32)


def two_parts(v):
    high = v.astype(BF16)
    return high, (v - high.astype(F32)).astype(BF16)


def place():
    col = lax.axis_index("col")
    return lax.axis_index("row"), col // 2, col % 2


def send_kernel(member_hbm, tests_hbm, points_hbm, targets_hbm, out_ref, packed_ref, wanted_ref,
                member_ref, tests_ref, sems):
    own_row, expert, _ = place()
    peers = member_hbm.shape[0]
    blocks_own, features, _ = tests_hbm.shape
    near = pl.multiple_of(expert // SUBLANES * SUBLANES, SUBLANES)
    copies = [
        pltpu.make_async_copy(member_hbm.at[:, pl.ds(near, SUBLANES), :], member_ref, sems.at[0]),
        pltpu.make_async_copy(tests_hbm, tests_ref, sems.at[1]),
        pltpu.make_async_copy(points_hbm.at[0], packed_ref.at[0:features], sems.at[2]),
        pltpu.make_async_copy(targets_hbm, packed_ref.at[features : features + 1], sems.at[3]),
    ]
    for c in copies:
        c.start()
    copies[0].wait()
    member = member_ref[...].astype(F32)
    sub = lax.broadcasted_iota(I32, member.shape, 1)
    mine = jnp.sum(jnp.where(sub == expert - near, member, 0.0), axis=1)
    lane = lax.broadcasted_iota(I32, mine.shape, 1)
    wanted = [
        jnp.sum(jnp.where(lane == own_row * blocks_own + b, mine, 0.0), axis=1, keepdims=True)
        for b in range(blocks_own)
    ]
    wide = [jnp.broadcast_to(w, (peers, LANES)) for w in wanted]
    for b in range(blocks_own):
        wanted_ref[b] = wide[b]
    copies[1].wait()
    blocks = [tests_ref[b] for b in range(blocks_own)]
    for r in range(peers):
        total = blocks[0] * wide[0][r : r + 1]
        for b in range(1, blocks_own):
            total = total + blocks[b] * wide[b][r : r + 1]
        out_ref[r] = total
    copies[2].wait()
    copies[3].wait()


def prepare_kernel(member_hbm, counts_hbm, own_f_hbm, own_ref, other_ref, other_f_ref,
                   aug_ref, fh_ref, fl_hbm, alpha_ref, slots_ref,
                   member_ref, counts_ref, own_f_ref, fl_ref, *rest, scale, step):
    cols_refs, sems = rest[:-1], rest[-1]
    own_row, expert, parity = place()
    half = own_ref.shape[1]
    features = scale[1]
    factor = scale[0]
    near = pl.multiple_of(expert // SUBLANES * SUBLANES, SUBLANES)
    chunks = half // step
    small = [
        pltpu.make_async_copy(counts_hbm, counts_ref, sems.at[0]),
        pltpu.make_async_copy(member_hbm.at[own_row, pl.ds(near, SUBLANES), :], member_ref, sems.at[1]),
    ]
    large = [
        pltpu.make_async_copy(
            own_f_hbm.at[0, step * a : step * a + step, 0 : 2 * step * (a + 1)],
            own_f_ref.at[step * a : step * a + step, 0 : 2 * step * (a + 1)],
            sems.at[2 + a],
        )
        for a in range(chunks)
    ]
    for c in small + large:
        c.start()
    small[0].wait()
    counts = counts_ref[...]
    lane = lax.broadcasted_iota(I32, counts.shape, 1)
    valid = jnp.sum(jnp.where(lane == expert, counts, 0).astype(F32), axis=1, keepdims=True)

    def columns(ref, odd):
        points, y = ref[0:features, :], ref[features : features + 1, :]
        where = 2 * lax.broadcasted_iota(I32, (1, half), 1) + odd
        alive = where.astype(F32) < valid
        scaled = jnp.where(alive, points * (2.0 * factor), 0.0)
        square = jnp.where(alive, -factor * jnp.sum(points * points, axis=0, keepdims=True), -1e9)
        xh, xm, xl = three_parts(scaled)
        sh, sm, sl = three_parts(square)
        row = lax.broadcasted_iota(I32, (features, half), 0)
        last = jnp.where(row == 0, sh, jnp.where(row == 1, sm, jnp.where(row == 2, sl, 0.0)))
        last = jnp.where((row >= 3) & (row < 6), 1.0, last)
        wide = [xh, xh, xm, xm, xh, xl, last, jnp.zeros_like(xh), jnp.broadcast_to(y, (LANES, half))]
        return jnp.concatenate(wide, axis=0).T

    own = columns(own_ref, parity)
    other = columns(other_ref, 1 - parity)
    first = jnp.where(parity == 0, own, other)
    second = jnp.where(parity == 0, other, own)
    for c, ref in enumerate(cols_refs):
        at = slice(c * LANES, c * LANES + LANES)
        ref[pl.ds(0, half, 2), :] = first[:, at]
        ref[pl.ds(1, half, 2), :] = second[:, at]
    aug_ref[:, 0:LANES] = cols_refs[0][...].astype(BF16)
    aug_ref[:, LANES : 2 * LANES] = cols_refs[1][...].astype(BF16)
    yh, yl = two_parts(cols_refs[2][...])

    small[1].wait()
    member = member_ref[...].astype(F32)
    sub = lax.broadcasted_iota(I32, member.shape, 0)
    mine = jnp.sum(jnp.where(sub == expert - near, member, 0.0), axis=0, keepdims=True)
    peers = slots_ref.shape[1]
    blocks_own = mine.shape[1] // peers
    row = lax.broadcasted_iota(I32, (peers, mine.shape[1]), 0)
    lane = lax.broadcasted_iota(I32, (peers, mine.shape[1]), 1)
    inside = (lane >= row * blocks_own) & (lane < row * blocks_own + blocks_own)
    held = jnp.sum(jnp.where(inside, mine, 0.0), axis=1, keepdims=True)
    before = jnp.sum(jnp.where(lane < row * blocks_own, mine, 0.0), axis=1, keepdims=True)
    for m in range(slots_ref.shape[0]):
        taken = (before == (2 * m + parity).astype(F32)) & (held > 0.5)
        slots_ref[m] = jnp.broadcast_to(jnp.where(taken, 1.0, 0.0), (peers, LANES))

    leaving = []
    sums = [jnp.zeros((SUBLANES, LANES), F32) for _ in range(2 * half // LANES)]
    for which in (1, 0):
        for a in range(chunks):
            reach = 2 * step * (a + 1)
            if which == 0:
                large[a].wait()
            src = (own_f_ref, other_f_ref)[which]
            to = slice(2 * step * a + step * which, 2 * step * a + step * which + step)
            f = src[step * a : step * a + step, 0:reach]
            fh, fl = two_parts(f)
            fh_ref[to, 0:reach] = fh
            fl_ref[to, 0:reach] = fl
            leaving.append(pltpu.make_async_copy(fl_ref.at[to, 0:reach], fl_hbm.at[to, 0:reach], sems.at[2 + chunks + len(leaving)]))
            leaving[-1].start()
            w = jnp.dot(fh, yh[0:reach], preferred_element_type=F32)
            w = w + jnp.dot(fh, yl[0:reach], preferred_element_type=F32)
            w = w + jnp.dot(fl, yh[0:reach], preferred_element_type=F32)
            for c in range(reach // LANES):
                part = f[:, c * LANES : c * LANES + LANES] * w
                sums[c] = sums[c] + jnp.sum(part.reshape(step // SUBLANES, SUBLANES, LANES), axis=0)
    for c, part in enumerate(sums):
        alpha = jnp.broadcast_to(jnp.sum(part, axis=0, keepdims=True), (LANES, LANES))
        alpha_ref[c * LANES : c * LANES + LANES, :] = alpha.T
    for c in leaving:
        c.wait()


def expert_kernel(aug_ref, fh_ref, fl_hbm, alpha_ref, slots_ref, tests_ref, out_ref, kh_ref, kl_ref, fl_ref, sems, *, scale, step):
    points = aug_ref.shape[0]
    coming = [
        pltpu.make_async_copy(
            fl_hbm.at[step * a : step * a + step, 0 : step * (a + 1)],
            fl_ref.at[step * a : step * a + step, 0 : step * (a + 1)],
            sems.at[a],
        )
        for a in range(points // step)
    ]
    for c in coming:
        c.start()
    slots, peers, _ = slots_ref.shape
    _, features, block = tests_ref.shape
    width = slots * block
    chosen = []
    for m in range(slots):
        s = slots_ref[m]
        total = tests_ref[0] * s[0:1]
        for r in range(1, peers):
            total = total + tests_ref[r] * s[r : r + 1]
        chosen.append(total)
    t = jnp.concatenate(chosen, axis=1)
    th, tm, tl = three_parts(t)
    square = -scale * jnp.sum(t * t, axis=0, keepdims=True)
    sh, sm, sl = three_parts(square)
    row = lax.broadcasted_iota(I32, (features, width), 0)
    last = jnp.where(row == 3, sh, jnp.where(row == 4, sm, jnp.where(row == 5, sl, 0.0)))
    last = jnp.where(row < 3, 1.0, last)
    taug = jnp.concatenate([th, tm, th, tm, tl, th, last, jnp.zeros_like(th)], axis=0).astype(BF16)
    quad = jnp.zeros((1, width), F32)
    mean = jnp.zeros((1, width), F32)
    for a in range(points // step):
        at = slice(a * step, a * step + step)
        k = jnp.exp2(jnp.dot(aug_ref[at, :], taug, preferred_element_type=F32))
        kh, kl = two_parts(k)
        kh_ref[at, :] = kh
        kl_ref[at, :] = kl
        mean = mean + jnp.sum(k * jnp.concatenate([alpha_ref[at, :]] * slots, axis=1), axis=0, keepdims=True)
    for a in range(points // step):
        at = slice(a * step, a * step + step)
        reach = step * (a + 1)
        solved = jnp.dot(fh_ref[at, 0:reach], kh_ref[0:reach, :], preferred_element_type=F32)
        coming[a].wait()
        solved = solved + jnp.dot(fl_ref[at, 0:reach], kh_ref[0:reach, :], preferred_element_type=F32)
        solved = solved + jnp.dot(fh_ref[at, 0:reach], kl_ref[0:reach, :], preferred_element_type=F32)
        quad = quad + jnp.sum(solved * solved, axis=0, keepdims=True)
    variance = NOISE + jnp.maximum(SIGNAL - quad, 0.0)
    gap = 0.5 * (math.log(SIGNAL + NOISE) - jnp.log(variance))
    weight = gap / variance
    both = jnp.concatenate([weight * mean, weight], axis=0)
    for r in range(peers):
        total = both[:, 0:block] * slots_ref[0, r : r + 1]
        for m in range(1, slots):
            total = total + both[:, m * block : m * block + block] * slots_ref[m, r : r + 1]
        out_ref[r] = total


def owner_kernel(wanted_ref, parts_ref, out_ref):
    peers, _, _ = parts_ref.shape
    blocks = wanted_ref.shape[0]
    num, wgt = [], []
    for b in range(blocks):
        total = parts_ref[0] * wanted_ref[b, 0:1]
        for r in range(1, peers):
            total = total + parts_ref[r] * wanted_ref[b, r : r + 1]
        num.append(total[0:1])
        wgt.append(total[1:2])
    tile = jnp.concatenate(num + wgt, axis=0)
    for j in range(out_ref.shape[0]):
        out_ref[j] = tile


def final_kernel(parts_ref, mean_ref, var_ref):
    parts = [parts_ref[j] for j in range(parts_ref.shape[0])]
    while len(parts) > 1:
        parts = [parts[i] + parts[i + 1] for i in range(0, len(parts), 2)]
    total = parts[0]
    blocks = mean_ref.shape[0]
    precision = 1.0 / (SIGNAL + NOISE) + total[blocks:]
    mean_ref[...] = total[0:blocks] / precision
    var_ref[...] = 1.0 / precision


def hbm(x):
    return pltpu.with_memory_space_constraint(x, pltpu.HBM)


def vmem(x):
    return pltpu.with_memory_space_constraint(x, pltpu.VMEM)


def on_device(train_points, targets, inverse_factor, counts, membership, test_points):
    cols = lax.axis_size("col")
    rows = lax.axis_size("row")
    slots = min(8, rows) // 2
    blocks_own, features, block = test_points.shape
    half = train_points.shape[2]
    points = 2 * half
    scale = math.log2(math.e) / features
    swap = [(i, i ^ 1) for i in range(cols)]
    step = 128
    in_hbm = pl.BlockSpec(memory_space=pltpu.HBM)
    in_vmem = pl.BlockSpec(memory_space=pltpu.VMEM)
    held = features + SUBLANES

    outgoing, packed, wanted = pl.pallas_call(
        send_kernel,
        out_shape=(pltpu.VMEM((rows, features, block), F32), pltpu.VMEM((held, half), F32), pltpu.VMEM((blocks_own, rows, LANES), F32)),
        in_specs=[in_hbm] * 4,
        out_specs=(in_vmem,) * 3,
        scratch_shapes=[pltpu.VMEM((rows, SUBLANES, membership.shape[2]), I32), pltpu.VMEM((blocks_own, features, block), F32), pltpu.SemaphoreType.DMA((4,))],
        compiler_params=pltpu.CompilerParams(vmem_limit_bytes=4 << 20),
        name="send",
    )(hbm(membership), hbm(test_points), hbm(train_points), hbm(targets))
    tests = lax.all_to_all(outgoing, "row", split_axis=0, concat_axis=0, tiled=True)
    other_factor = lax.ppermute(inverse_factor[0], "col", swap)
    other = lax.ppermute(packed, "col", swap)

    aug, fh, fl, alpha, table = pl.pallas_call(
        lambda *refs: prepare_kernel(*refs, scale=(scale, features), step=step),
        out_shape=(
            pltpu.VMEM((points, 2 * LANES), BF16),
            pltpu.VMEM((points, points), BF16),
            pltpu.HBM((points, points), BF16),
            pltpu.VMEM((points, LANES), F32),
            pltpu.VMEM((slots, rows, LANES), F32),
        ),
        in_specs=[in_hbm] * 3 + [in_vmem] * 3,
        out_specs=(in_vmem, in_vmem, in_hbm, in_vmem, in_vmem),
        scratch_shapes=[
            pltpu.VMEM((SUBLANES, membership.shape[2]), I32),
            pltpu.VMEM(counts.shape, I32),
            pltpu.VMEM((half, points), F32),
            pltpu.VMEM((points, points), BF16),
            pltpu.VMEM((points, LANES), F32),
            pltpu.VMEM((points, LANES), F32),
            pltpu.VMEM((points, LANES), F32),
            pltpu.SemaphoreType.DMA((2 + 3 * (half // step),)),
        ],
        compiler_params=pltpu.CompilerParams(vmem_limit_bytes=20 << 20),
        name="prepare",
    )(hbm(membership), hbm(counts), hbm(inverse_factor), vmem(packed), vmem(other), vmem(other_factor))
    parts = pl.pallas_call(
        lambda *refs: expert_kernel(*refs, scale=scale, step=2 * step),
        out_shape=pltpu.VMEM((rows, 2, block), F32),
        in_specs=[in_vmem] * 2 + [in_hbm] + [in_vmem] * 3,
        out_specs=in_vmem,
        scratch_shapes=[pltpu.VMEM((points, slots * block), BF16)] * 2 + [pltpu.VMEM((points, points), BF16), pltpu.SemaphoreType.DMA((half // step,))],
        compiler_params=pltpu.CompilerParams(vmem_limit_bytes=16 << 20),
        name="expert",
    )(vmem(aug), vmem(fh), hbm(fl), vmem(alpha), vmem(table), vmem(tests))
    arrived = lax.all_to_all(parts, "row", split_axis=0, concat_axis=0, tiled=True)
    spread = pl.pallas_call(
        owner_kernel,
        out_shape=pltpu.VMEM((cols, 2 * blocks_own, block), F32),
        in_specs=[in_vmem] * 2,
        out_specs=in_vmem,
        compiler_params=pltpu.CompilerParams(vmem_limit_bytes=4 << 20),
        name="owner",
    )(vmem(wanted), vmem(arrived))
    shares = lax.all_to_all(spread, "col", split_axis=0, concat_axis=0, tiled=True)
    return pl.pallas_call(
        final_kernel,
        out_shape=(jax.ShapeDtypeStruct((blocks_own, block), F32),) * 2,
        in_specs=[in_vmem],
        out_specs=(in_vmem,) * 2,
        compiler_params=pltpu.CompilerParams(vmem_limit_bytes=4 << 20),
        name="final",
    )(vmem(shares))


def solution(mesh):
    in_specs = (
        P("row", None, "col"),
        P("row", "col"),
        P("row", "col", None),
        P("row", None),
        P(),
        P("row", None, None),
    )
    out_specs = (P("row", None), P("row", None))

    return jax.shard_map(on_device, mesh=mesh, in_specs=in_specs, out_specs=out_specs, check_vma=False)
```

time: 102 us -> 79.2 us (0.78)
  matrix products: 17.6 us -> 0 us
  local copies, waits for them, and re-layouts: 15.3 us -> 2.89 us
  Pallas kernels: 0 us -> 10 us
  waiting for transfers between devices: 1.13 us -> 6.94 us
  other arithmetic: 5.55 us -> 0 us
  blocking collectives: 39.8 us -> 37.6 us
    dot_general x10 -> x0, matrix products: 17.6 us -> none  [the longest x2 4.52 us: cross_kernel(): products = jnp.einsum('dn,dp->np', train_cols, test_cols, precision=HIGHEST)]
    pallas_call x0 -> x5, Pallas kernels: none -> 10 us  [the longest x1 3.88 us: on_device(): pl.pallas_call(lambda *refs: prepare_kernel(*refs, scale=(scale, features...]
    dynamic_slice x5 -> x0, local copies, waits for them, and re-layouts: 8.17 us -> none  [the longest x2 4.28 us: on_device(): lax.dynamic_index_in_dim(factor_pairs, 1 - parity, 2, keepdims=False)]
    ppermute x2, starting transfers between devices: 4.77 us -> 10.9 us  [the longest x1 8.75 us: on_device(): other_factor = lax.ppermute(inverse_factor[0], 'col', swap)]
    all_to_all x1, starting transfers between devices: 15.7 us -> 9.58 us  [on_device(): lax.all_to_all(outgoing, 'row', split_axis=0, concat_axis=0, tiled=True)]
    all_to_all x1, waiting for transfers between devices: 0.01 us -> 5.97 us  [on_device(): lax.all_to_all(outgoing, 'row', split_axis=0, concat_axis=0, tiled=True)]
    another operation x2 -> x0, local copies, waits for them, and re-layouts: 2.6 us -> none  [the longest x1 2.5 us: on_device(): factor_pairs = inverse_factor[0].reshape(rows_half, rows_half, 2)]
    all_to_all x2, blocking collectives: 39.8 us -> 37.6 us  [the longest x1 21.2 us: on_device(): lax.all_to_all(parts, 'row', split_axis=0, concat_axis=0, tiled=True)]
  transfers between devices with their start and end apart: 3 -> 3, of which waited for: 1 -> 2; matrix products, arithmetic and copies ran while one was open for 20% -> 0% of each run, Pallas kernels for 0% -> 5%
where the time goes in v1:
time: 79.2 us; the launch traced here: 78.7 us
  blocking collectives  37.6 us (47%)
  starting transfers between devices  20.5 us (26%)
  Pallas kernels  10 us (13%)
  waiting for transfers between devices  6.94 us (9%)
  local copies, waits for them, and re-layouts  2.89 us (4%)
    all_to_all x1, blocking collectives, on_device(): lax.all_to_all(parts, 'row', split_axis=0, concat_axis=0, tiled=True)  21.2 us
    all_to_all x1, blocking collectives, on_device(): lax.all_to_all(spread, 'col', split_axis=0, concat_axis=0, tiled=True)  16.5 us
    all_to_all x1, starting transfers between devices, on_device(): lax.all_to_all(outgoing, 'row', split_axis=0, concat_axis=0, tiled=True)  9.58 us
    ppermute x1, starting transfers between devices, on_device(): other_factor = lax.ppermute(inverse_factor[0], 'col', swap)  8.75 us
    all_to_all x1, waiting for transfers between devices, on_device(): lax.all_to_all(outgoing, 'row', split_axis=0, concat_axis=0, tiled=True)  5.97 us
    pallas_call x1, Pallas kernels, on_device(): pl.pallas_call(lambda *refs: prepare_kernel(*refs, scale=(scale, features...  3.88 us
    pallas_call x1, Pallas kernels, on_device(): pl.pallas_call(lambda *refs: expert_kernel(*refs, scale=scale, step=2 * s...  3.73 us
    unnamed x4, local copies, waits for them, and re-layouts  2.89 us
  transfers between devices with their start and end apart: 3, of which 2 were waited for; matrix products, arithmetic and copies ran while one was open for 0% of the time, Pallas kernels for 5%

profile of v1, /device:TPU:1, one launch (start us, length us, event | category | flops | bytes accessed | tf_op | source)
XLA Modules:
  0.0 78.7 jit_solution(10668403449564544115)
XLA Ops:
  0.6 8.7 %collective-permute-start.1 = (f32[512,1024]{1,0:T(8,128)}, f32[512,1024]{1,0:T(8,128)S(1)}, u32[]{:S(2)}, u32[]{:S(2)}) collective-permute-start(f32[512,1024]{1,0:T(8,128)} %bitcast.1), channel_id=1, source_target_pairs={{0,1},{1,0},{2,3},{3,2},{4,5},{5,4},{6,7},{7,6},{8,9},{9,8},{10,11... | collective-permute-start | bytes 6291464 | tf_op jit(solution)/shard_map/ppermute | solution.py:287
  9.4 1.8 %send.1 = (f32[16,32,128]{2,1,0:T(8,128)}, f32[40,512]{1,0:T(8,128)S(1)}, f32[4,16,128]{2,1,0:T(8,128)S(1)}) custom-call(s32[16,16,64]{2,1,0:T(8,128)} %refs_0_.1, f32[4,32,128]{2,1,0:T(8,128)} %tests_hbm.1, f32[1,32,512]{2,1,0:T(8,128)} %points_hbm.1, f32[1,512]{1,0:T(1,128)} %targets_hbm.1), custom_call_target="tpu_custom_call" | custom-call | tf_op jit(solution)/shard_map/send/pallas_call | solution.py:277
  11.2 9.6 %all-to-all-start = ((f32[16,32,128]{2,1,0:T(8,128)}), f32[16,32,128]{2,1,0:T(8,128)S(1)}, u32[]{:S(2)}, u32[]{:S(2)}) async-start(f32[16,32,128]{2,1,0:T(8,128)} %get-tuple-element.17), calls=%async_computation | async-start | bytes 524288 | tf_op jit(solution)/shard_map/all_to_all | solution.py:286
  20.8 2.2 %collective-permute-start = (f32[40,512]{1,0:T(8,128)S(1)}, f32[40,512]{1,0:T(8,128)S(1)}, u32[]{:S(2)}, u32[]{:S(2)}) collective-permute-start(f32[40,512]{1,0:T(8,128)S(1)} %get-tuple-element.11.refs_3_), channel_id=1, source_target_pairs={{0,1},{1,0},{2,3},{3,2},{4,5},{5,4},{6,7},{7,6},{8,9},{9,8},{10,11... | collective-permute-start | bytes 245768 | tf_op jit(solution)/shard_map/ppermute | solution.py:288
  23.0 1.0 %collective-permute-done.refs_4_ = f32[40,512]{1,0:T(8,128)S(1)} collective-permute-done((f32[40,512]{1,0:T(8,128)S(1)}, f32[40,512]{1,0:T(8,128)S(1)}, u32[]{:S(2)}, u32[]{:S(2)}) %collective-permute-start) | collective-permute-done | bytes 81952 | tf_op jit(solution)/shard_map/ppermute | solution.py:288
  23.9 0.0 collective-permute-done.1.refs_5_
  23.9 3.9 %prepare.1 = (bf16[1024,256]{1,0:T(8,128)(2,1)S(1)}, bf16[1024,1024]{1,0:T(8,128)(2,1)S(1)}, bf16[1024,1024]{1,0:T(8,128)(2,1)}, f32[1024,128]{1,0:T(8,128)S(1)}, f32[4,16,128]{2,1,0:T(8,128)S(1)}) custom-call(s32[16,16,64]{2,1,0:T(8,128)} %refs_0_.1, s32[1,16]{1,0:T(1,128)} %refs_1_.1, f32[1,512,1024]{2,1,0:T(8,128)} %refs_2_.1, ...), custom_call_target="tpu_custom_call" | custom-call | tf_op jit(solution)/shard_map/prepare/pallas_call | solution.py:290
  27.8 0.0 copy-start
  27.9 1.3 %copy-done = bf16[1024,1024]{1,0:T(8,128)(2,1)} copy-done((bf16[1024,1024]{1,0:T(8,128)(2,1)}, bf16[1024,1024]{1,0:T(8,128)(2,1)S(1)}, u32[]{:S(2)}) %copy-start) | copy-done | bytes 2097176
  29.1 6.0 %all-to-all-done.refs_5_ = f32[16,32,128]{2,1,0:T(8,128)S(1)} async-done(((f32[16,32,128]{2,1,0:T(8,128)}), f32[16,32,128]{2,1,0:T(8,128)S(1)}, u32[]{:S(2)}, u32[]{:S(2)}) %all-to-all-start) | async-done | bytes 262176 | tf_op jit(solution)/shard_map/all_to_all | solution.py:286
  35.1 0.0 copy-start.1
  35.1 1.6 %copy-done.1 = bf16[1024,1024]{1,0:T(8,128)(2,1)S(1)} copy-done((bf16[1024,1024]{1,0:T(8,128)(2,1)S(1)}, bf16[1024,1024]{1,0:T(8,128)(2,1)}, u32[]{:S(2)}) %copy-start.1) | copy-done | bytes 2097176
  36.7 3.7 %expert.1 = f32[16,2,128]{2,1,0:T(2,128)S(1)} custom-call(bf16[1024,256]{1,0:T(8,128)(2,1)S(1)} %get-tuple-element.12.refs_0_, bf16[1024,1024]{1,0:T(8,128)(2,1)S(1)} %copy-done.1, bf16[1024,1024]{1,0:T(8,128)(2,1)} %get-tuple-element.14.refs_2_, f32[1024,128]{1,0:T(8,128)S(1)} %get-tuple-element.15.refs_3_, f32[4,16,128]{2,1,0:T(8,128)S(1)} %get-tuple-element.16.refs_4_, ...), custom_call_target="tpu_custom_call" | custom-call | tf_op jit(solution)/shard_map/expert/pallas_call | solution.py:314
  40.5 21.2 %all_to_all.15.parts_ref = f32[16,2,128]{2,1,0:T(2,128)S(1)} all-to-all(f32[16,2,128]{2,1,0:T(2,128)S(1)} %expert.1), channel_id=1, replica_groups=mesh['row'=16,'col'=32] {'row'}, dimensions={0} | all-to-all | bytes 32768 | tf_op jit(solution)/shard_map/all_to_all | solution.py:323
  61.7 16.5 %all_to_all.16.parts_ref = f32[32,8,128]{2,1,0:T(8,128)S(1)} all-to-all(f32[32,8,128]{2,1,0:T(8,128)S(1)} %owner.1), channel_id=1, replica_groups=mesh['row'=16,'col'=32] {'col'}, dimensions={0} | all-to-all | bytes 262144 | tf_op jit(solution)/shard_map/all_to_all | solution.py:332
  78.1 0.6 final.1
  (1 shorter events, 0.0 us)
Async XLA Ops:
  0.6 23.3 %collective-permute-start.1 = (f32[512,1024]{1,0:T(8,128)}, f32[512,1024]{1,0:T(8,128)S(1)}, u32[]{:S(2)}, u32[]{:S(2)}) collective-permute-start(f32[512,1024]{1,0:T(8,128)} %bitcast.1), channel_id=1, source_target_pairs={{0,1},{1,0},{2,3},{3,2},{4,5},{5,4},{6,7},{7,6},{8,9},{9,8},{10,11... | collective-permute-start | bytes 6291464 | tf_op jit(solution)/shard_map/ppermute | solution.py:287
  11.2 23.9 %all-to-all-start = ((f32[16,32,128]{2,1,0:T(8,128)}), f32[16,32,128]{2,1,0:T(8,128)S(1)}, u32[]{:S(2)}, u32[]{:S(2)}) async-start(f32[16,32,128]{2,1,0:T(8,128)} %get-tuple-element.17), calls=%async_computation | async-start | bytes 524288 | tf_op jit(solution)/shard_map/all_to_all | solution.py:286
  20.8 3.2 %collective-permute-start = (f32[40,512]{1,0:T(8,128)S(1)}, f32[40,512]{1,0:T(8,128)S(1)}, u32[]{:S(2)}, u32[]{:S(2)}) collective-permute-start(f32[40,512]{1,0:T(8,128)S(1)} %get-tuple-element.11.refs_3_), channel_id=1, source_target_pairs={{0,1},{1,0},{2,3},{3,2},{4,5},{5,4},{6,7},{7,6},{8,9},{9,8},{10,11... | collective-permute-start | bytes 245768 | tf_op jit(solution)/shard_map/ppermute | solution.py:288
  27.8 1.3 %copy-start = (bf16[1024,1024]{1,0:T(8,128)(2,1)}, bf16[1024,1024]{1,0:T(8,128)(2,1)S(1)}, u32[]{:S(2)}) copy-start(bf16[1024,1024]{1,0:T(8,128)(2,1)S(1)} %get-tuple-element.13.refs_1_) | copy-start | bytes 6291460
  35.1 1.6 %copy-start.1 = (bf16[1024,1024]{1,0:T(8,128)(2,1)S(1)}, bf16[1024,1024]{1,0:T(8,128)(2,1)}, u32[]{:S(2)}) copy-start(bf16[1024,1024]{1,0:T(8,128)(2,1)} %copy-done) | copy-start | bytes 6291460

commit v2 on v1

--- a/solution.py
+++ b/solution.py
@@ -70,31 +70,23 @@
     copies[3].wait()
 
 
-def prepare_kernel(member_hbm, counts_hbm, own_f_hbm, own_ref, other_ref, other_f_ref,
-                   aug_ref, fh_ref, fl_hbm, alpha_ref, slots_ref,
-                   member_ref, counts_ref, own_f_ref, fl_ref, *rest, scale, step):
-    cols_refs, sems = rest[:-1], rest[-1]
+def first_column(a, step):
+    return step * a * (a + 1)
+
+
+def points_kernel(member_hbm, counts_hbm, own_ref, other_ref, aug_ref, y_ref, slots_ref,
+                  member_ref, counts_ref, first_ref, second_ref, third_ref, sems, *, features, factor):
     own_row, expert, parity = place()
     half = own_ref.shape[1]
-    features = scale[1]
-    factor = scale[0]
     near = pl.multiple_of(expert // SUBLANES * SUBLANES, SUBLANES)
-    chunks = half // step
-    small = [
+    copies = [
         pltpu.make_async_copy(counts_hbm, counts_ref, sems.at[0]),
         pltpu.make_async_copy(member_hbm.at[own_row, pl.ds(near, SUBLANES), :], member_ref, sems.at[1]),
     ]
-    large = [
-        pltpu.make_async_copy(
-            own_f_hbm.at[0, step * a : step * a + step, 0 : 2 * step * (a + 1)],
-            own_f_ref.at[step * a : step * a + step, 0 : 2 * step * (a + 1)],
-            sems.at[2 + a],
-        )
-        for a in range(chunks)
-    ]
-    for c in small + large:
+    for c in copies:
         c.start()
-    small[0].wait()
+    for c in copies:
+        c.wait()
     counts = counts_ref[...]
     lane = lax.broadcasted_iota(I32, counts.shape, 1)
     valid = jnp.sum(jnp.where(lane == expert, counts, 0).astype(F32), axis=1, keepdims=True)
@@ -111,21 +103,22 @@
         last = jnp.where(row == 0, sh, jnp.where(row == 1, sm, jnp.where(row == 2, sl, 0.0)))
         last = jnp.where((row >= 3) & (row < 6), 1.0, last)
         wide = [xh, xh, xm, xm, xh, xl, last, jnp.zeros_like(xh), jnp.broadcast_to(y, (LANES, half))]
-        return jnp.concatenate(wide, axis=0).T
+        return jnp.concatenate(wide, axis=0)
 
     own = columns(own_ref, parity)
     other = columns(other_ref, 1 - parity)
     first = jnp.where(parity == 0, own, other)
     second = jnp.where(parity == 0, other, own)
-    for c, ref in enumerate(cols_refs):
+    for c, ref in enumerate((first_ref, second_ref, third_ref)):
         at = slice(c * LANES, c * LANES + LANES)
-        ref[pl.ds(0, half, 2), :] = first[:, at]
-        ref[pl.ds(1, half, 2), :] = second[:, at]
-    aug_ref[:, 0:LANES] = cols_refs[0][...].astype(BF16)
-    aug_ref[:, LANES : 2 * LANES] = cols_refs[1][...].astype(BF16)
-    yh, yl = two_parts(cols_refs[2][...])
-
-    small[1].wait()
+        ref[pl.ds(0, half, 2), :] = first[at].T
+        ref[pl.ds(1, half, 2), :] = second[at].T
+    aug_ref[:, 0:LANES] = first_ref[...].astype(BF16)
+    aug_ref[:, LANES : 2 * LANES] = second_ref[...].astype(BF16)
+    yh, yl = two_parts(third_ref[...])
+    y_ref[0] = yh
+    y_ref[1] = yl
+
     member = member_ref[...].astype(F32)
     sub = lax.broadcasted_iota(I32, member.shape, 0)
     mine = jnp.sum(jnp.where(sub == expert - near, member, 0.0), axis=0, keepdims=True)
@@ -140,46 +133,45 @@
         taken = (before == (2 * m + parity).astype(F32)) & (held > 0.5)
         slots_ref[m] = jnp.broadcast_to(jnp.where(taken, 1.0, 0.0), (peers, LANES))
 
-    leaving = []
+
+def factor_kernel(own_f_hbm, other_f_ref, y_ref, fh_ref, fl_ref, alpha_ref, own_f_ref, sems, *, step):
+    half = own_f_ref.shape[0]
+    chunks = half // step
+    coming = [
+        pltpu.make_async_copy(
+            own_f_hbm.at[0, step * a : step * a + step, 0 : 2 * step * (a + 1)],
+            own_f_ref.at[step * a : step * a + step, 0 : 2 * step * (a + 1)],
+            sems.at[a],
+        )
+        for a in range(chunks)
+    ]
+    for c in coming:
+        c.start()
     sums = [jnp.zeros((SUBLANES, LANES), F32) for _ in range(2 * half // LANES)]
     for which in (1, 0):
         for a in range(chunks):
             reach = 2 * step * (a + 1)
             if which == 0:
-                large[a].wait()
+                coming[a].wait()
             src = (own_f_ref, other_f_ref)[which]
-            to = slice(2 * step * a + step * which, 2 * step * a + step * which + step)
+            to = slice(step * which, step * which + step)
+            at = slice(first_column(a, step), first_column(a, step) + reach)
             f = src[step * a : step * a + step, 0:reach]
             fh, fl = two_parts(f)
-            fh_ref[to, 0:reach] = fh
-            fl_ref[to, 0:reach] = fl
-            leaving.append(pltpu.make_async_copy(fl_ref.at[to, 0:reach], fl_hbm.at[to, 0:reach], sems.at[2 + chunks + len(leaving)]))
-            leaving[-1].start()
-            w = jnp.dot(fh, yh[0:reach], preferred_element_type=F32)
-            w = w + jnp.dot(fh, yl[0:reach], preferred_element_type=F32)
-            w = w + jnp.dot(fl, yh[0:reach], preferred_element_type=F32)
+            fh_ref[to, at] = fh
+            fl_ref[to, at] = fl
+            w = jnp.dot(fh, y_ref[0, 0:reach], preferred_element_type=F32)
+            w = w + jnp.dot(fh, y_ref[1, 0:reach], preferred_element_type=F32)
+            w = w + jnp.dot(fl, y_ref[0, 0:reach], preferred_element_type=F32)
             for c in range(reach // LANES):
                 part = f[:, c * LANES : c * LANES + LANES] * w
                 sums[c] = sums[c] + jnp.sum(part.reshape(step // SUBLANES, SUBLANES, LANES), axis=0)
     for c, part in enumerate(sums):
-        alpha = jnp.broadcast_to(jnp.sum(part, axis=0, keepdims=True), (LANES, LANES))
-        alpha_ref[c * LANES : c * LANES + LANES, :] = alpha.T
-    for c in leaving:
-        c.wait()
-
-
-def expert_kernel(aug_ref, fh_ref, fl_hbm, alpha_ref, slots_ref, tests_ref, out_ref, kh_ref, kl_ref, fl_ref, sems, *, scale, step):
+        alpha_ref[:, c * LANES : c * LANES + LANES] = jnp.broadcast_to(jnp.sum(part, axis=0, keepdims=True), (SUBLANES, LANES))
+
+
+def expert_kernel(aug_ref, fh_ref, fl_ref, alpha_ref, slots_ref, tests_ref, out_ref, kh_ref, kl_ref, *, scale, step):
     points = aug_ref.shape[0]
-    coming = [
-        pltpu.make_async_copy(
-            fl_hbm.at[step * a : step * a + step, 0 : step * (a + 1)],
-            fl_ref.at[step * a : step * a + step, 0 : step * (a + 1)],
-            sems.at[a],
-        )
-        for a in range(points // step)
-    ]
-    for c in coming:
-        c.start()
     slots, peers, _ = slots_ref.shape
     _, features, block = tests_ref.shape
     width = slots * block
@@ -206,14 +198,20 @@
         kh, kl = two_parts(k)
         kh_ref[at, :] = kh
         kl_ref[at, :] = kl
-        mean = mean + jnp.sum(k * jnp.concatenate([alpha_ref[at, :]] * slots, axis=1), axis=0, keepdims=True)
+        alpha = jnp.concatenate(
+            [
+                jnp.broadcast_to(alpha_ref[0:1, c : c + LANES], (LANES, LANES)).T
+                for c in range(a * step, a * step + step, LANES)
+            ],
+            axis=0,
+        )
+        mean = mean + jnp.sum(k * jnp.concatenate([alpha] * slots, axis=1), axis=0, keepdims=True)
     for a in range(points // step):
-        at = slice(a * step, a * step + step)
         reach = step * (a + 1)
-        solved = jnp.dot(fh_ref[at, 0:reach], kh_ref[0:reach, :], preferred_element_type=F32)
-        coming[a].wait()
-        solved = solved + jnp.dot(fl_ref[at, 0:reach], kh_ref[0:reach, :], preferred_element_type=F32)
-        solved = solved + jnp.dot(fh_ref[at, 0:reach], kl_ref[0:reach, :], preferred_element_type=F32)
+        at = slice(first_column(a, step // 2), first_column(a, step // 2) + reach)
+        solved = jnp.dot(fh_ref[:, at], kh_ref[0:reach, :], preferred_element_type=F32)
+        solved = solved + jnp.dot(fl_ref[:, at], kh_ref[0:reach, :], preferred_element_type=F32)
+        solved = solved + jnp.dot(fh_ref[:, at], kl_ref[0:reach, :], preferred_element_type=F32)
         quad = quad + jnp.sum(solved * solved, axis=0, keepdims=True)
     variance = NOISE + jnp.maximum(SIGNAL - quad, 0.0)
     gap = 0.5 * (math.log(SIGNAL + NOISE) - jnp.log(variance))
@@ -284,42 +282,52 @@
         name="send",
     )(hbm(membership), hbm(test_points), hbm(train_points), hbm(targets))
     tests = lax.all_to_all(outgoing, "row", split_axis=0, concat_axis=0, tiled=True)
+    other = lax.ppermute(packed, "col", swap)
     other_factor = lax.ppermute(inverse_factor[0], "col", swap)
-    other = lax.ppermute(packed, "col", swap)
-
-    aug, fh, fl, alpha, table = pl.pallas_call(
-        lambda *refs: prepare_kernel(*refs, scale=(scale, features), step=step),
+
+    aug, y, table = pl.pallas_call(
+        lambda *refs: points_kernel(*refs, features=features, factor=scale),
         out_shape=(
             pltpu.VMEM((points, 2 * LANES), BF16),
-            pltpu.VMEM((points, points), BF16),
-            pltpu.HBM((points, points), BF16),
-            pltpu.VMEM((points, LANES), F32),
+            pltpu.VMEM((2, points, LANES), BF16),
             pltpu.VMEM((slots, rows, LANES), F32),
         ),
-        in_specs=[in_hbm] * 3 + [in_vmem] * 3,
-        out_specs=(in_vmem, in_vmem, in_hbm, in_vmem, in_vmem),
+        in_specs=[in_hbm] * 2 + [in_vmem] * 2,
+        out_specs=(in_vmem,) * 3,
         scratch_shapes=[
             pltpu.VMEM((SUBLANES, membership.shape[2]), I32),
             pltpu.VMEM(counts.shape, I32),
-            pltpu.VMEM((half, points), F32),
-            pltpu.VMEM((points, points), BF16),
             pltpu.VMEM((points, LANES), F32),
             pltpu.VMEM((points, LANES), F32),
             pltpu.VMEM((points, LANES), F32),
-            pltpu.SemaphoreType.DMA((2 + 3 * (half // step),)),
+            pltpu.SemaphoreType.DMA((2,)),
         ],
-        compiler_params=pltpu.CompilerParams(vmem_limit_bytes=20 << 20),
-        name="prepare",
-    )(hbm(membership), hbm(counts), hbm(inverse_factor), vmem(packed), vmem(other), vmem(other_factor))
+        compiler_params=pltpu.CompilerParams(vmem_limit_bytes=16 << 20),
+        name="points",
+    )(hbm(membership), hbm(counts), vmem(packed), vmem(other))
+    held_factor = (2 * step, first_column(half // step, step))
+    fh, fl, alpha = pl.pallas_call(
+        lambda *refs: factor_kernel(*refs, step=step),
+        out_shape=(
+            pltpu.VMEM(held_factor, BF16),
+            pltpu.VMEM(held_factor, BF16),
+            pltpu.VMEM((SUBLANES, points), F32),
+        ),
+        in_specs=[in_hbm] + [in_vmem] * 2,
+        out_specs=(in_vmem,) * 3,
+        scratch_shapes=[pltpu.VMEM((half, points), F32), pltpu.SemaphoreType.DMA((half // step,))],
+        compiler_params=pltpu.CompilerParams(vmem_limit_bytes=16 << 20),
+        name="factor",
+    )(hbm(inverse_factor), vmem(other_factor), vmem(y))
     parts = pl.pallas_call(
         lambda *refs: expert_kernel(*refs, scale=scale, step=2 * step),
         out_shape=pltpu.VMEM((rows, 2, block), F32),
-        in_specs=[in_vmem] * 2 + [in_hbm] + [in_vmem] * 3,
+        in_specs=[in_vmem] * 6,
         out_specs=in_vmem,
-        scratch_shapes=[pltpu.VMEM((points, slots * block), BF16)] * 2 + [pltpu.VMEM((points, points), BF16), pltpu.SemaphoreType.DMA((half // step,))],
+        scratch_shapes=[pltpu.VMEM((points, slots * block), BF16)] * 2,
         compiler_params=pltpu.CompilerParams(vmem_limit_bytes=16 << 20),
         name="expert",
-    )(vmem(aug), vmem(fh), hbm(fl), vmem(alpha), vmem(table), vmem(tests))
+    )(vmem(aug), vmem(fh), vmem(fl), vmem(alpha), vmem(table), vmem(tests))
     arrived = lax.all_to_all(parts, "row", split_axis=0, concat_axis=0, tiled=True)
     spread = pl.pallas_call(
         owner_kernel,

time: 79.2 us -> 79.9 us (level)
  local copies, waits for them, and re-layouts: 2.89 us -> 4.26 us
    unnamed x4 -> x8, local copies, waits for them, and re-layouts: 2.89 us -> 4.26 us
    pallas_call x1 -> x2, Pallas kernels: 3.88 us -> 3.48 us  [the longest x1 2.15 us: on_device(): pl.pallas_call(lambda *refs: factor_kernel(*refs, step=step), out_shape=(...]
  transfers between devices with their start and end apart: 3 -> 3, of which waited for: 2 -> 2; matrix products, arithmetic and copies ran while one was open for 0% -> 0% of each run, Pallas kernels for 5% -> 4%
where the time goes in v2:
time: 79.9 us; the launch traced here: 79.4 us
  blocking collectives  37.6 us (47%)
  starting transfers between devices  20.6 us (26%)
  Pallas kernels  9.47 us (12%)
  waiting for transfers between devices  6.78 us (8%)
  local copies, waits for them, and re-layouts  4.26 us (5%)
    all_to_all x1, blocking collectives, on_device(): lax.all_to_all(parts, 'row', split_axis=0, concat_axis=0, tiled=True)  21.2 us
    all_to_all x1, blocking collectives, on_device(): lax.all_to_all(spread, 'col', split_axis=0, concat_axis=0, tiled=True)  16.5 us
    all_to_all x1, starting transfers between devices, on_device(): lax.all_to_all(outgoing, 'row', split_axis=0, concat_axis=0, tiled=True)  9.63 us
    ppermute x1, starting transfers between devices, on_device(): other_factor = lax.ppermute(inverse_factor[0], 'col', swap)  8.75 us
    all_to_all x1, waiting for transfers between devices, on_device(): lax.all_to_all(outgoing, 'row', split_axis=0, concat_axis=0, tiled=True)  5.82 us
    unnamed x8, local copies, waits for them, and re-layouts  4.26 us
    pallas_call x1, Pallas kernels, on_device(): pl.pallas_call(lambda *refs: expert_kernel(*refs, scale=scale, step=2 * s...  3.56 us
    ppermute x1, starting transfers between devices, on_device(): other = lax.ppermute(packed, 'col', swap)  2.2 us
  transfers between devices with their start and end apart: 3, of which 2 were waited for; matrix products, arithmetic and copies ran while one was open for 0% of the time, Pallas kernels for 4%

profile of v2, /device:TPU:1, one launch (start us, length us, event | category | flops | bytes accessed | tf_op | source)
XLA Modules:
  0.0 79.4 jit_solution(258963682303115093)
XLA Ops:
  0.6 8.7 %collective-permute-start.1 = (f32[512,1024]{1,0:T(8,128)}, f32[512,1024]{1,0:T(8,128)S(1)}, u32[]{:S(2)}, u32[]{:S(2)}) collective-permute-start(f32[512,1024]{1,0:T(8,128)} %bitcast.1), channel_id=1, source_target_pairs={{0,1},{1,0},{2,3},{3,2},{4,5},{5,4},{6,7},{7,6},{8,9},{9,8},{10,11... | collective-permute-start | bytes 6291464 | tf_op jit(solution)/shard_map/ppermute | solution.py:286
  9.4 1.8 %send.1 = (f32[16,32,128]{2,1,0:T(8,128)}, f32[40,512]{1,0:T(8,128)S(1)}, f32[4,16,128]{2,1,0:T(8,128)S(1)}) custom-call(s32[16,16,64]{2,1,0:T(8,128)} %refs_0_.2, f32[4,32,128]{2,1,0:T(8,128)} %tests_hbm.1, f32[1,32,512]{2,1,0:T(8,128)} %points_hbm.1, f32[1,512]{1,0:T(1,128)} %targets_hbm.1), custom_call_target="tpu_custom_call" | custom-call | tf_op jit(solution)/shard_map/send/pallas_call | solution.py:275
  11.2 9.6 %all-to-all-start = ((f32[16,32,128]{2,1,0:T(8,128)}), f32[16,32,128]{2,1,0:T(8,128)}, u32[]{:S(2)}, u32[]{:S(2)}) async-start(f32[16,32,128]{2,1,0:T(8,128)} %get-tuple-element.19), calls=%async_computation | async-start | bytes 524288 | tf_op jit(solution)/shard_map/all_to_all | solution.py:284
  20.8 2.2 %collective-permute-start = (f32[40,512]{1,0:T(8,128)S(1)}, f32[40,512]{1,0:T(8,128)S(1)}, u32[]{:S(2)}, u32[]{:S(2)}) collective-permute-start(f32[40,512]{1,0:T(8,128)S(1)} %get-tuple-element.12.refs_2_), channel_id=1, source_target_pairs={{0,1},{1,0},{2,3},{3,2},{4,5},{5,4},{6,7},{7,6},{8,9},{9,8},{10,11... | collective-permute-start | bytes 245768 | tf_op jit(solution)/shard_map/ppermute | solution.py:285
  23.0 1.0 %collective-permute-done.refs_3_ = f32[40,512]{1,0:T(8,128)S(1)} collective-permute-done((f32[40,512]{1,0:T(8,128)S(1)}, f32[40,512]{1,0:T(8,128)S(1)}, u32[]{:S(2)}, u32[]{:S(2)}) %collective-permute-start) | collective-permute-done | bytes 81952 | tf_op jit(solution)/shard_map/ppermute | solution.py:285
  24.0 1.3 %points.1 = (bf16[1024,256]{1,0:T(8,128)(2,1)S(1)}, bf16[2,1024,128]{2,1,0:T(8,128)(2,1)S(1)}, f32[4,16,128]{2,1,0:T(8,128)S(1)}) custom-call(s32[16,16,64]{2,1,0:T(8,128)} %refs_0_.2, s32[1,16]{1,0:T(1,128)} %refs_1_.1, f32[40,512]{1,0:T(8,128)S(1)} %get-tuple-element.12.refs_2_, f32[40,512]{1,0:T(8,128)S(1)} %collective-permute-done.refs_3_), custom_call_target="tpu_custom_call" | custom-call | tf_op jit(solution)/shard_map/points/pallas_call | solution.py:288
  25.3 0.0 copy-start.2
  25.3 0.8 %copy-done.2 = bf16[1024,256]{1,0:T(8,128)(2,1)} copy-done((bf16[1024,256]{1,0:T(8,128)(2,1)}, bf16[1024,256]{1,0:T(8,128)(2,1)S(1)}, u32[]{:S(2)}) %copy-start.2) | copy-done | bytes 524312
  26.1 0.0 collective-permute-done.1.refs_1_
  26.2 2.1 %factor.1 = (bf16[256,2560]{1,0:T(8,128)(2,1)S(1)}, bf16[256,2560]{1,0:T(8,128)(2,1)S(1)}, f32[8,1024]{1,0:T(8,128)S(1)}) custom-call(f32[1,512,1024]{2,1,0:T(8,128)} %refs_0_.3, f32[512,1024]{1,0:T(8,128)S(1)} %collective-permute-done.1.refs_1_, bf16[2,1024,128]{2,1,0:T(8,128)(2,1)S(1)} %get-tuple-element.14.refs_2_), custom_call_target="tpu_custom_call" | custom-call | tf_op jit(solution)/shard_map/factor/pallas_call | solution.py:309
  28.3 0.0 copy-start
  28.3 1.1 %copy-done = bf16[256,2560]{1,0:T(8,128)(2,1)} copy-done((bf16[256,2560]{1,0:T(8,128)(2,1)}, bf16[256,2560]{1,0:T(8,128)(2,1)S(1)}, u32[]{:S(2)}) %copy-start) | copy-done | bytes 1310744
  29.4 5.8 %all-to-all-done.refs_5_ = f32[16,32,128]{2,1,0:T(8,128)} async-done(((f32[16,32,128]{2,1,0:T(8,128)}), f32[16,32,128]{2,1,0:T(8,128)}, u32[]{:S(2)}, u32[]{:S(2)}) %all-to-all-start) | async-done | bytes 262176 | tf_op jit(solution)/shard_map/all_to_all | solution.py:284
  35.2 0.0 copy-start.1
  35.2 1.3 %copy-done.1 = bf16[256,2560]{1,0:T(8,128)(2,1)S(1)} copy-done((bf16[256,2560]{1,0:T(8,128)(2,1)S(1)}, bf16[256,2560]{1,0:T(8,128)(2,1)}, u32[]{:S(2)}) %copy-start.1) | copy-done | bytes 1310744
  36.5 0.0 copy-start.3
  36.5 1.0 %copy-done.3 = bf16[1024,256]{1,0:T(8,128)(2,1)S(1)} copy-done((bf16[1024,256]{1,0:T(8,128)(2,1)S(1)}, bf16[1024,256]{1,0:T(8,128)(2,1)}, u32[]{:S(2)}) %copy-start.3) | copy-done | bytes 524312
  37.6 3.6 %expert.1 = f32[16,2,128]{2,1,0:T(2,128)S(1)} custom-call(bf16[1024,256]{1,0:T(8,128)(2,1)S(1)} %copy-done.3, bf16[256,2560]{1,0:T(8,128)(2,1)S(1)} %get-tuple-element.15.refs_1_, bf16[256,2560]{1,0:T(8,128)(2,1)S(1)} %copy-done.1, f32[8,1024]{1,0:T(8,128)S(1)} %get-tuple-element.17.refs_3_, f32[4,16,128]{2,1,0:T(8,128)S(1)} %get-tuple-element.18.refs_4_, ...), custom_call_target="tpu_custom_call" | custom-call | tf_op jit(solution)/shard_map/expert/pallas_call | solution.py:322
  41.2 21.2 %all_to_all.15.parts_ref = f32[16,2,128]{2,1,0:T(2,128)S(1)} all-to-all(f32[16,2,128]{2,1,0:T(2,128)S(1)} %expert.1), channel_id=1, replica_groups=mesh['row'=16,'col'=32] {'row'}, dimensions={0} | all-to-all | bytes 32768 | tf_op jit(solution)/shard_map/all_to_all | solution.py:331
  62.4 16.5 %all_to_all.16.parts_ref = f32[32,8,128]{2,1,0:T(8,128)S(1)} all-to-all(f32[32,8,128]{2,1,0:T(8,128)S(1)} %owner.1), channel_id=1, replica_groups=mesh['row'=16,'col'=32] {'col'}, dimensions={0} | all-to-all | bytes 262144 | tf_op jit(solution)/shard_map/all_to_all | solution.py:340
  78.8 0.6 final.1
  (1 shorter events, 0.0 us)
Async XLA Ops:
  0.6 25.5 %collective-permute-start.1 = (f32[512,1024]{1,0:T(8,128)}, f32[512,1024]{1,0:T(8,128)S(1)}, u32[]{:S(2)}, u32[]{:S(2)}) collective-permute-start(f32[512,1024]{1,0:T(8,128)} %bitcast.1), channel_id=1, source_target_pairs={{0,1},{1,0},{2,3},{3,2},{4,5},{5,4},{6,7},{7,6},{8,9},{9,8},{10,11... | collective-permute-start | bytes 6291464 | tf_op jit(solution)/shard_map/ppermute | solution.py:286
  11.2 24.0 %all-to-all-start = ((f32[16,32,128]{2,1,0:T(8,128)}), f32[16,32,128]{2,1,0:T(8,128)}, u32[]{:S(2)}, u32[]{:S(2)}) async-start(f32[16,32,128]{2,1,0:T(8,128)} %get-tuple-element.19), calls=%async_computation | async-start | bytes 524288 | tf_op jit(solution)/shard_map/all_to_all | solution.py:284
  20.8 3.2 %collective-permute-start = (f32[40,512]{1,0:T(8,128)S(1)}, f32[40,512]{1,0:T(8,128)S(1)}, u32[]{:S(2)}, u32[]{:S(2)}) collective-permute-start(f32[40,512]{1,0:T(8,128)S(1)} %get-tuple-element.12.refs_2_), channel_id=1, source_target_pairs={{0,1},{1,0},{2,3},{3,2},{4,5},{5,4},{6,7},{7,6},{8,9},{9,8},{10,11... | collective-permute-start | bytes 245768 | tf_op jit(solution)/shard_map/ppermute | solution.py:285
  25.3 0.8 %copy-start.2 = (bf16[1024,256]{1,0:T(8,128)(2,1)}, bf16[1024,256]{1,0:T(8,128)(2,1)S(1)}, u32[]{:S(2)}) copy-start(bf16[1024,256]{1,0:T(8,128)(2,1)S(1)} %get-tuple-element.13.refs_0_) | copy-start | bytes 1572868
  28.3 1.1 %copy-start = (bf16[256,2560]{1,0:T(8,128)(2,1)}, bf16[256,2560]{1,0:T(8,128)(2,1)S(1)}, u32[]{:S(2)}) copy-start(bf16[256,2560]{1,0:T(8,128)(2,1)S(1)} %get-tuple-element.16.refs_2_) | copy-start | bytes 3932164
  35.2 1.3 %copy-start.1 = (bf16[256,2560]{1,0:T(8,128)(2,1)S(1)}, bf16[256,2560]{1,0:T(8,128)(2,1)}, u32[]{:S(2)}) copy-start(bf16[256,2560]{1,0:T(8,128)(2,1)} %copy-done) | copy-start | bytes 3932164
  36.5 1.0 %copy-start.3 = (bf16[1024,256]{1,0:T(8,128)(2,1)S(1)}, bf16[1024,256]{1,0:T(8,128)(2,1)}, u32[]{:S(2)}) copy-start(bf16[1024,256]{1,0:T(8,128)(2,1)} %copy-done.2) | copy-start | bytes 1572868

commit v3 on v2

v3 whole, which is shorter than its diff:
```python
import math

import jax
import jax.numpy as jnp
from jax import lax
from jax.experimental import pallas as pl
from jax.experimental.pallas import tpu as pltpu
from jax.sharding import PartitionSpec as P

SIGNAL = 1.0
NOISE = 0.1
BF16 = jnp.bfloat16
F32 = jnp.float32
I32 = jnp.int32
LANES = 128
SUBLANES = 8
GROUP = 4


def three_parts(v):
    high = v.astype(BF16).astype(F32)
    rest = v - high
    mid = rest.astype(BF16).astype(F32)
    return high, mid, (rest - mid).astype(BF16).astype(F32)


def two_parts(v):
    high = v.astype(BF16)
    return high, (v - high.astype(F32)).astype(BF16)


def place():
    col = lax.axis_index("col")
    return lax.axis_index("row"), col // 2, col % 2


def send_kernel(member_hbm, counts_hbm, tests_hbm, points_hbm, targets_hbm,
                out_hbm, packed_ref, wanted_ref, slots_ref, valid_ref,
                member_ref, counts_ref, tests_ref, out_ref, sems):
    own_row, expert, parity = place()
    peers = member_hbm.shape[0]
    features = points_hbm.shape[1]
    blocks_own, part, _ = tests_ref.shape
    near = pl.multiple_of(expert // SUBLANES * SUBLANES, SUBLANES)
    mine_at = pl.multiple_of(parity * part, part)
    copies = [
        pltpu.make_async_copy(member_hbm.at[:, pl.ds(near, SUBLANES), :], member_ref, sems.at[0]),
        pltpu.make_async_copy(tests_hbm.at[:, pl.ds(mine_at, part), :], tests_ref, sems.at[1]),
        pltpu.make_async_copy(counts_hbm, counts_ref, sems.at[2]),
        pltpu.make_async_copy(points_hbm.at[0], packed_ref.at[0:features], sems.at[3]),
        pltpu.make_async_copy(targets_hbm, packed_ref.at[features : features + 1], sems.at[4]),
    ]
    for c in copies:
        c.start()
    copies[0].wait()
    member = member_ref[...].astype(F32)
    sub = lax.broadcasted_iota(I32, member.shape, 1)
    mine = jnp.sum(jnp.where(sub == expert - near, member, 0.0), axis=1)
    row = lax.broadcasted_iota(I32, mine.shape, 0)
    lane = lax.broadcasted_iota(I32, mine.shape, 1)
    wide = [
        jnp.broadcast_to(
            jnp.sum(jnp.where(lane == own_row * blocks_own + b, mine, 0.0), axis=1, keepdims=True), (peers, LANES)
        )
        for b in range(blocks_own)
    ]
    for b in range(blocks_own):
        wanted_ref[b] = wide[b]
    copies[1].wait()
    blocks = [tests_ref[b] for b in range(blocks_own)]
    for r in range(peers):
        total = blocks[0] * wide[0][r : r + 1]
        for b in range(1, blocks_own):
            total = total + blocks[b] * wide[b][r : r + 1]
        out_ref[r] = total
        if r % GROUP == GROUP - 1:
            at = slice(r + 1 - GROUP, r + 1)
            copies.append(pltpu.make_async_copy(out_ref.at[at], out_hbm.at[at], sems.at[len(copies)]))
            copies[-1].start()
    own = jnp.sum(jnp.where(row == own_row, mine, 0.0), axis=0, keepdims=True)
    inside = (lane >= row * blocks_own) & (lane < row * blocks_own + blocks_own)
    held = jnp.sum(jnp.where(inside, own, 0.0), axis=1, keepdims=True)
    before = jnp.sum(jnp.where(lane < row * blocks_own, own, 0.0), axis=1, keepdims=True)
    for s in range(slots_ref.shape[0]):
        taken = (before == float(s)) & (held > 0.5)
        slots_ref[s] = jnp.broadcast_to(jnp.where(taken, 1.0, 0.0), (peers, LANES))
    copies[2].wait()
    counts = counts_ref[...]
    lane = lax.broadcasted_iota(I32, counts.shape, 1)
    valid = jnp.sum(jnp.where(lane == expert, counts, 0).astype(F32), axis=1, keepdims=True)
    valid_ref[...] = jnp.broadcast_to(valid, valid_ref.shape)
    for c in copies[3:]:
        c.wait()


def pick_kernel(slots_ref, tests_ref, mine_ref, theirs_ref):
    _, _, parity = place()
    peers, _, block = tests_ref.shape
    for m in range(slots_ref.shape[0] // 2):
        for odd, ref in ((parity, mine_ref), (1 - parity, theirs_ref)):
            s = slots_ref[2 * m + odd]
            total = tests_ref[0] * s[0:1]
            for r in range(1, peers):
                total = total + tests_ref[r] * s[r : r + 1]
            ref[:, m * block : m * block + block] = total


def first_column(a, step):
    return step * a * (a + 1)


def factor_copies(f_hbm, f_ref, sems, step):
    blocks = [(slice(step * a, step * a + step), slice(0, 2 * step * (a + 1))) for a in range(f_ref.shape[0] // step)]
    return [pltpu.make_async_copy(f_hbm.at[(0, *at)], f_ref.at[at], sems.at[a]) for a, at in enumerate(blocks)]


def factor_block(f_ref, a, step):
    return f_ref[step * a : step * a + step, 0 : 2 * step * (a + 1)]


def add_alpha(sums, f, parts, y_ref):
    rows, reach = f.shape
    w = jnp.dot(parts[0], y_ref[0:reach], preferred_element_type=F32)
    w = w + jnp.dot(parts[1], y_ref[0:reach], preferred_element_type=F32)
    w = w + pltpu.roll(w, LANES // 2, 1)
    for c in range(reach // LANES):
        part = f[:, c * LANES : c * LANES + LANES] * w
        sums[c] = sums[c] + jnp.sum(part.reshape(rows // SUBLANES, SUBLANES, LANES), axis=0)


def points_kernel(valid_ref, own_ref, other_ref, f_hbm, aug_ref, y_ref, alpha_ref,
                  first_ref, second_ref, third_ref, f_ref, sems, *, features, factor, step):
    _, _, parity = place()
    half = own_ref.shape[1]
    coming = factor_copies(f_hbm, f_ref, sems, step)
    for c in coming:
        c.start()
    valid = valid_ref[0:1, 0:1]

    def columns(ref, odd):
        points, y = ref[0:features, :], ref[features : features + 1, :]
        where = 2 * lax.broadcasted_iota(I32, (1, half), 1) + odd
        alive = where.astype(F32) < valid
        scaled = jnp.where(alive, points * (2.0 * factor), 0.0)
        square = jnp.where(alive, -factor * jnp.sum(points * points, axis=0, keepdims=True), -1e9)
        xh, xm, xl = three_parts(scaled)
        sh, sm, sl = three_parts(square)
        row = lax.broadcasted_iota(I32, (features, half), 0)
        last = jnp.where(row == 0, sh, jnp.where(row == 1, sm, jnp.where(row == 2, sl, 0.0)))
        last = jnp.where((row >= 3) & (row < 6), 1.0, last)
        wide = [xh, xh, xm, xm, xh, xl, last, jnp.zeros_like(xh), jnp.broadcast_to(y, (LANES, half))]
        return jnp.concatenate(wide, axis=0)

    own = columns(own_ref, parity)
    other = columns(other_ref, 1 - parity)
    first = jnp.where(parity == 0, own, other)
    second = jnp.where(parity == 0, other, own)
    for c, ref in enumerate((first_ref, second_ref, third_ref)):
        at = slice(c * LANES, c * LANES + LANES)
        ref[pl.ds(0, half, 2), :] = first[at].T
        ref[pl.ds(1, half, 2), :] = second[at].T
    aug_ref[:, 0:LANES] = first_ref[...].astype(BF16)
    aug_ref[:, LANES : 2 * LANES] = second_ref[...].astype(BF16)
    y = third_ref[...]
    yh = y.astype(BF16).astype(F32)
    lane = lax.broadcasted_iota(I32, y.shape, 1)
    y_ref[...] = jnp.where(lane < LANES // 2, yh, y - yh).astype(BF16)
    sums = [jnp.zeros((SUBLANES, LANES), F32) for _ in range(2 * half // LANES)]
    for a, c in enumerate(coming):
        c.wait()
        f = factor_block(f_ref, a, step)
        add_alpha(sums, f, two_parts(f), y_ref)
    for c, part in enumerate(sums):
        alpha_ref[:, c * LANES : c * LANES + LANES] = part


def factor_kernel(own_f_hbm, other_f_ref, y_ref, own_alpha_ref, fh_ref, fl_ref, alpha_ref, own_f_ref, sems, *, step):
    coming = factor_copies(own_f_hbm, own_f_ref, sems, step)
    for c in coming:
        c.start()
    sums = [own_alpha_ref[:, c : c + LANES] for c in range(0, y_ref.shape[0], LANES)]
    for which, f_ref in ((1, other_f_ref), (0, own_f_ref)):
        rows = slice(step * which, step * which + step)
        for a, c in enumerate(coming):
            if which == 0:
                c.wait()
            f = factor_block(f_ref, a, step)
            parts = two_parts(f)
            at = slice(first_column(a, step), first_column(a + 1, step))
            fh_ref[rows, at], fl_ref[rows, at] = parts
            if which == 1:
                add_alpha(sums, f, parts, y_ref)
    for c, part in enumerate(sums):
        alpha_ref[:, c * LANES : c * LANES + LANES] = jnp.broadcast_to(jnp.sum(part, axis=0, keepdims=True), (SUBLANES, LANES))


def expert_kernel(aug_ref, fh_ref, fl_ref, alpha_ref, slots_ref, mine_ref, theirs_ref, out_ref, kh_ref, kl_ref, *, scale, step):
    _, _, parity = place()
    points = aug_ref.shape[0]
    peers = slots_ref.shape[1]
    slots = slots_ref.shape[0] // 2
    part, width = mine_ref.shape
    features, block = 2 * part, width // slots
    mine, theirs = mine_ref[...], theirs_ref[...]
    t = jnp.concatenate([jnp.where(parity == 0, mine, theirs), jnp.where(parity == 0, theirs, mine)], axis=0)
    th, tm, tl = three_parts(t)
    square = -scale * jnp.sum(t * t, axis=0, keepdims=True)
    sh, sm, sl = three_parts(square)
    row = lax.broadcasted_iota(I32, (features, width), 0)
    last = jnp.where(row == 3, sh, jnp.where(row == 4, sm, jnp.where(row == 5, sl, 0.0)))
    last = jnp.where(row < 3, 1.0, last)
    taug = jnp.concatenate([th, tm, th, tm, tl, th, last, jnp.zeros_like(th)], axis=0).astype(BF16)
    quad = jnp.zeros((1, width), F32)
    mean = jnp.zeros((1, width), F32)
    for a in range(points // step):
        at = slice(a * step, a * step + step)
        k = jnp.exp2(jnp.dot(aug_ref[at, :], taug, preferred_element_type=F32))
        kh, kl = two_parts(k)
        kh_ref[at, :] = kh
        kl_ref[at, :] = kl
        alpha = jnp.concatenate(
            [
                jnp.broadcast_to(alpha_ref[0:1, c : c + LANES], (LANES, LANES)).T
                for c in range(a * step, a * step + step, LANES)
            ],
            axis=0,
        )
        mean = mean + jnp.sum(k * jnp.concatenate([alpha] * slots, axis=1), axis=0, keepdims=True)
    for a in range(points // step):
        reach = step * (a + 1)
        at = slice(first_column(a, step // 2), first_column(a, step // 2) + reach)
        solved = jnp.dot(fh_ref[:, at], kh_ref[0:reach, :], preferred_element_type=F32)
        solved = solved + jnp.dot(fl_ref[:, at], kh_ref[0:reach, :], preferred_element_type=F32)
        solved = solved + jnp.dot(fh_ref[:, at], kl_ref[0:reach, :], preferred_element_type=F32)
        quad = quad + jnp.sum(solved * solved, axis=0, keepdims=True)
    variance = NOISE + jnp.maximum(SIGNAL - quad, 0.0)
    gap = 0.5 * (math.log(SIGNAL + NOISE) - jnp.log(variance))
    weight = gap / variance
    both = jnp.concatenate([weight * mean, weight], axis=0)
    for r in range(peers):
        total = both[:, 0:block] * slots_ref[parity, r : r + 1]
        for m in range(1, slots):
            total = total + both[:, m * block : m * block + block] * slots_ref[2 * m + parity, r : r + 1]
        out_ref[r] = total


def owner_kernel(wanted_ref, parts_ref, out_ref):
    peers, _, _ = parts_ref.shape
    blocks = wanted_ref.shape[0]
    num, wgt = [], []
    for b in range(blocks):
        total = parts_ref[0] * wanted_ref[b, 0:1]
        for r in range(1, peers):
            total = total + parts_ref[r] * wanted_ref[b, r : r + 1]
        num.append(total[0:1])
        wgt.append(total[1:2])
    tile = jnp.concatenate(num + wgt, axis=0)
    for j in range(out_ref.shape[0]):
        out_ref[j] = tile


def final_kernel(parts_ref, mean_ref, var_ref):
    parts = [parts_ref[j] for j in range(parts_ref.shape[0])]
    while len(parts) > 1:
        parts = [parts[i] + parts[i + 1] for i in range(0, len(parts), 2)]
    total = parts[0]
    blocks = mean_ref.shape[0]
    precision = 1.0 / (SIGNAL + NOISE) + total[blocks:]
    mean_ref[...] = total[0:blocks] / precision
    var_ref[...] = 1.0 / precision


def hbm(x):
    return pltpu.with_memory_space_constraint(x, pltpu.HBM)


def vmem(x):
    return pltpu.with_memory_space_constraint(x, pltpu.VMEM)


def on_device(train_points, targets, inverse_factor, counts, membership, test_points):
    cols = lax.axis_size("col")
    rows = lax.axis_size("row")
    slots = min(8, rows) // 2
    blocks_own, features, block = test_points.shape
    half = train_points.shape[2]
    points = 2 * half
    scale = math.log2(math.e) / features
    swap = [(i, i ^ 1) for i in range(cols)]
    step = 128
    in_hbm = pl.BlockSpec(memory_space=pltpu.HBM)
    in_vmem = pl.BlockSpec(memory_space=pltpu.VMEM)
    held = features + SUBLANES

    outgoing, packed, wanted, table, valid = pl.pallas_call(
        send_kernel,
        out_shape=(
            pltpu.HBM((rows, features // 2, block), F32),
            pltpu.VMEM((held, half), F32),
            pltpu.VMEM((blocks_own, rows, LANES), F32),
            pltpu.VMEM((2 * slots, rows, LANES), F32),
            pltpu.VMEM((SUBLANES, LANES), F32),
        ),
        in_specs=[in_hbm] * 5,
        out_specs=(in_hbm,) + (in_vmem,) * 4,
        scratch_shapes=[
            pltpu.VMEM((rows, SUBLANES, membership.shape[2]), I32),
            pltpu.VMEM(counts.shape, I32),
            pltpu.VMEM((blocks_own, features // 2, block), F32),
            pltpu.VMEM((rows, features // 2, block), F32),
            pltpu.SemaphoreType.DMA((5 + rows // GROUP,)),
        ],
        compiler_params=pltpu.CompilerParams(vmem_limit_bytes=4 << 20),
        name="send",
    )(hbm(membership), hbm(counts), hbm(test_points), hbm(train_points), hbm(targets))
    tests = lax.all_to_all(outgoing, "row", split_axis=0, concat_axis=0, tiled=True)
    other = lax.ppermute(packed, "col", swap)
    other_factor = lax.ppermute(inverse_factor[0], "col", swap)

    chunks = half // step
    reach = first_column(chunks, step)
    held_f = [pltpu.VMEM((half, points), F32), pltpu.SemaphoreType.DMA((chunks,))]
    aug, y, own_alpha = pl.pallas_call(
        lambda *refs: points_kernel(*refs, features=features, factor=scale, step=step),
        out_shape=(
            pltpu.VMEM((points, 2 * LANES), BF16),
            pltpu.VMEM((points, LANES), BF16),
            pltpu.VMEM((SUBLANES, points), F32),
        ),
        in_specs=[in_vmem] * 3 + [in_hbm],
        out_specs=(in_vmem,) * 3,
        scratch_shapes=[pltpu.VMEM((points, LANES), F32)] * 3 + held_f,
        compiler_params=pltpu.CompilerParams(vmem_limit_bytes=16 << 20),
        name="points",
    )(vmem(valid), vmem(packed), vmem(other), hbm(inverse_factor))
    tests, aug = lax.optimization_barrier((tests, aug))
    mine, theirs = pl.pallas_call(
        pick_kernel,
        out_shape=(pltpu.VMEM((features // 2, slots * block), F32),) * 2,
        in_specs=[in_vmem] * 2,
        out_specs=(in_vmem,) * 2,
        compiler_params=pltpu.CompilerParams(vmem_limit_bytes=4 << 20),
        name="pick",
    )(vmem(table), vmem(tests))
    theirs = lax.ppermute(theirs, "col", swap)
    fh, fl, alpha = pl.pallas_call(
        lambda *refs: factor_kernel(*refs, step=step),
        out_shape=(
            pltpu.VMEM((2 * step, reach), BF16),
            pltpu.VMEM((2 * step, reach), BF16),
            pltpu.VMEM((SUBLANES, points), F32),
        ),
        in_specs=[in_hbm] + [in_vmem] * 3,
        out_specs=(in_vmem,) * 3,
        scratch_shapes=held_f,
        compiler_params=pltpu.CompilerParams(vmem_limit_bytes=12 << 20),
        name="factor",
    )(hbm(inverse_factor), vmem(other_factor), vmem(y), vmem(own_alpha))
    parts = pl.pallas_call(
        lambda *refs: expert_kernel(*refs, scale=scale, step=2 * step),
        out_shape=pltpu.VMEM((rows, 2, block), F32),
        in_specs=[in_vmem] * 7,
        out_specs=in_vmem,
        scratch_shapes=[pltpu.VMEM((points, slots * block), BF16)] * 2,
        compiler_params=pltpu.CompilerParams(vmem_limit_bytes=16 << 20),
        name="expert",
    )(*map(vmem, (aug, fh, fl, alpha, table, mine, theirs)))
    arrived = lax.all_to_all(parts, "row", split_axis=0, concat_axis=0, tiled=True)
    spread = pl.pallas_call(
        owner_kernel,
        out_shape=pltpu.VMEM((cols, 2 * blocks_own, block), F32),
        in_specs=[in_vmem] * 2,
        out_specs=in_vmem,
        compiler_params=pltpu.CompilerParams(vmem_limit_bytes=4 << 20),
        name="owner",
    )(vmem(wanted), vmem(arrived))
    shares = lax.all_to_all(spread, "col", split_axis=0, concat_axis=0, tiled=True)
    return pl.pallas_call(
        final_kernel,
        out_shape=(jax.ShapeDtypeStruct((blocks_own, block), F32),) * 2,
        in_specs=[in_vmem],
        out_specs=(in_vmem,) * 2,
        compiler_params=pltpu.CompilerParams(vmem_limit_bytes=4 << 20),
        name="final",
    )(vmem(shares))


def solution(mesh):
    in_specs = (
        P("row", None, "col"),
        P("row", "col"),
        P("row", "col", None),
        P("row", None),
        P(),
        P("row", None, None),
    )
    out_specs = (P("row", None), P("row", None))

    return jax.shard_map(on_device, mesh=mesh, in_specs=in_specs, out_specs=out_specs, check_vma=False)
```

time: 79.9 us -> 74.2 us (0.929)
  blocking collectives: 37.6 us -> 32 us
  local copies, waits for them, and re-layouts: 4.26 us -> 0 us
  starting transfers between devices: 20.6 us -> 24.4 us
  waiting for transfers between devices: 6.78 us -> 7.76 us
    all_to_all x1, blocking collectives: 21.2 us -> 16 us  [on_device(): lax.all_to_all(parts, 'row', split_axis=0, concat_axis=0, tiled=True)]
    unnamed x8 -> x0, local copies, waits for them, and re-layouts: 4.26 us -> none
    ppermute x0 -> x1, starting transfers between devices: none -> 3.88 us  [on_device(): theirs = lax.ppermute(theirs, 'col', swap)]
    pallas_call x1, Pallas kernels: 1.33 us -> 2.42 us  [on_device(): pl.pallas_call(lambda *refs: points_kernel(*refs, features=features, fact...]
    pallas_call x1, Pallas kernels: 3.56 us -> 2.56 us  [on_device(): pl.pallas_call(lambda *refs: expert_kernel(*refs, scale=scale, step=2 * s...]
    all_to_all x1, waiting for transfers between devices: 5.82 us -> 6.79 us  [on_device(): lax.all_to_all(outgoing, 'row', split_axis=0, concat_axis=0, tiled=True)]
    pallas_call x1 -> x2, Pallas kernels: 1.78 us -> 1.81 us  [the longest x1 1.72 us: on_device(): pl.pallas_call(send_kernel, out_shape=(pltpu.HBM((rows, features // 2, bl...]
  transfers between devices with their start and end apart: 3 -> 4, of which waited for: 2 -> 2; matrix products, arithmetic and copies ran while one was open for 0% -> 0% of each run, Pallas kernels for 4% -> 5%
where the time goes in v3:
time: 74.2 us; the launch traced here: 73.8 us
  blocking collectives  32 us (43%)
  starting transfers between devices  24.4 us (33%)
  Pallas kernels  8.89 us (12%)
  waiting for transfers between devices  7.76 us (10%)
    all_to_all x1, blocking collectives, on_device(): lax.all_to_all(parts, 'row', split_axis=0, concat_axis=0, tiled=True)  16 us
    all_to_all x1, blocking collectives, on_device(): lax.all_to_all(spread, 'col', split_axis=0, concat_axis=0, tiled=True)  15.9 us
    all_to_all x1, starting transfers between devices, on_device(): lax.all_to_all(outgoing, 'row', split_axis=0, concat_axis=0, tiled=True)  9.58 us
    ppermute x1, starting transfers between devices, on_device(): other_factor = lax.ppermute(inverse_factor[0], 'col', swap)  8.75 us
    all_to_all x1, waiting for transfers between devices, on_device(): lax.all_to_all(outgoing, 'row', split_axis=0, concat_axis=0, tiled=True)  6.79 us
    ppermute x1, starting transfers between devices, on_device(): theirs = lax.ppermute(theirs, 'col', swap)  3.88 us
    pallas_call x1, Pallas kernels, on_device(): pl.pallas_call(lambda *refs: expert_kernel(*refs, scale=scale, step=2 * s...  2.56 us
    pallas_call x1, Pallas kernels, on_device(): pl.pallas_call(lambda *refs: points_kernel(*refs, features=features, fact...  2.42 us
  transfers between devices with their start and end apart: 4, of which 2 were waited for; matrix products, arithmetic and copies ran while one was open for 0% of the time, Pallas kernels for 5%

profile of v3, /device:TPU:1, one launch (start us, length us, event | category | flops | bytes accessed | tf_op | source)
XLA Modules:
  0.0 73.8 jit_solution(17674872068624950993)
XLA Ops:
  0.6 8.7 %collective-permute-start.1 = (f32[512,1024]{1,0:T(8,128)}, f32[512,1024]{1,0:T(8,128)S(1)}, u32[]{:S(2)}, u32[]{:S(2)}) collective-permute-start(f32[512,1024]{1,0:T(8,128)} %bitcast.1), channel_id=1, source_target_pairs={{0,1},{1,0},{2,3},{3,2},{4,5},{5,4},{6,7},{7,6},{8,9},{9,8},{10,11... | collective-permute-start | bytes 6291464 | tf_op jit(solution)/shard_map/ppermute | solution.py:318
  9.4 1.7 %send.1 = (f32[16,16,128]{2,1,0:T(8,128)}, f32[40,512]{1,0:T(8,128)S(1)}, f32[4,16,128]{2,1,0:T(8,128)S(1)}, f32[8,16,128]{2,1,0:T(8,128)S(1)}, f32[8,128]{1,0:T(8,128)S(1)}) custom-call(s32[16,16,64]{2,1,0:T(8,128)} %member_hbm.1, s32[1,16]{1,0:T(1,128)} %counts_hbm.1, f32[4,32,128]{2,1,0:T(8,128)} %tests_hbm.1, f32[1,32,512]{2,1,0:T(8,128)} %points_hbm.1, ...), custom_call_target="tpu_custom_call" | custom-call | tf_op jit(solution)/shard_map/send/pallas_call | solution.py:295
  11.1 9.6 %all-to-all-start = ((f32[16,16,128]{2,1,0:T(8,128)}), f32[16,16,128]{2,1,0:T(8,128)S(1)}, u32[]{:S(2)}, u32[]{:S(2)}) async-start(f32[16,16,128]{2,1,0:T(8,128)} %get-tuple-element.18), calls=%async_computation | async-start | bytes 262144 | tf_op jit(solution)/shard_map/all_to_all | solution.py:316
  20.7 2.2 %collective-permute-start = (f32[40,512]{1,0:T(8,128)S(1)}, f32[40,512]{1,0:T(8,128)S(1)}, u32[]{:S(2)}, u32[]{:S(2)}) collective-permute-start(f32[40,512]{1,0:T(8,128)S(1)} %get-tuple-element.20.refs_1_), channel_id=1, source_target_pairs={{0,1},{1,0},{2,3},{3,2},{4,5},{5,4},{6,7},{7,6},{8,9},{9,8},{10,11... | collective-permute-start | bytes 245768 | tf_op jit(solution)/shard_map/ppermute | solution.py:317
  22.9 1.0 %collective-permute-done.refs_2_ = f32[40,512]{1,0:T(8,128)S(1)} collective-permute-done((f32[40,512]{1,0:T(8,128)S(1)}, f32[40,512]{1,0:T(8,128)S(1)}, u32[]{:S(2)}, u32[]{:S(2)}) %collective-permute-start) | collective-permute-done | bytes 81952 | tf_op jit(solution)/shard_map/ppermute | solution.py:317
  23.9 2.4 %points.1 = (bf16[1024,256]{1,0:T(8,128)(2,1)S(1)}, bf16[1024,128]{1,0:T(8,128)(2,1)S(1)}, f32[8,1024]{1,0:T(8,128)S(1)}) custom-call(f32[8,128]{1,0:T(8,128)S(1)} %get-tuple-element.19.refs_0_, f32[40,512]{1,0:T(8,128)S(1)} %get-tuple-element.20.refs_1_, f32[40,512]{1,0:T(8,128)S(1)} %collective-permute-done.refs_2_, f32[1,512,1024]{2,1,0:T(8,128)} %refs_0_.1), custom_call_target="tpu_custom_call" | custom-call | tf_op jit(solution)/shard_map/points/pallas_call | solution.py:323
  26.3 6.8 %all-to-all-done.tests_ref = f32[16,16,128]{2,1,0:T(8,128)S(1)} async-done(((f32[16,16,128]{2,1,0:T(8,128)}), f32[16,16,128]{2,1,0:T(8,128)S(1)}, u32[]{:S(2)}, u32[]{:S(2)}) %all-to-all-start) | async-done | bytes 131104 | tf_op jit(solution)/shard_map/all_to_all | solution.py:316
  33.1 0.1 pick.1
  33.2 3.9 %collective-permute-start.2 = (f32[16,512]{1,0:T(8,128)S(1)}, f32[16,512]{1,0:T(8,128)S(1)}, u32[]{:S(2)}, u32[]{:S(2)}) collective-permute-start(f32[16,512]{1,0:T(8,128)S(1)} %get-tuple-element.31), channel_id=1, source_target_pairs={{0,1},{1,0},{2,3},{3,2},{4,5},{5,4},{6,7},{7,6},{8,9},{9,8},{10,11... | collective-permute-start | bytes 98312 | tf_op jit(solution)/shard_map/ppermute | solution.py:345
  37.1 0.0 collective-permute-done.1.refs_1_
  37.1 1.5 %factor.1 = (bf16[256,2560]{1,0:T(8,128)(2,1)S(1)}, bf16[256,2560]{1,0:T(8,128)(2,1)S(1)}, f32[8,1024]{1,0:T(8,128)S(1)}) custom-call(f32[1,512,1024]{2,1,0:T(8,128)} %refs_0_.1, f32[512,1024]{1,0:T(8,128)S(1)} %collective-permute-done.1.refs_1_, bf16[1024,128]{1,0:T(8,128)(2,1)S(1)} %get-tuple-element.23.refs_2_, f32[8,1024]{1,0:T(8,128)S(1)} %get-tuple-element.24.refs_3_), custom_call_target="tpu_custom_call" | custom-call | tf_op jit(solution)/shard_map/factor/pallas_call | solution.py:346
  38.6 0.0 collective-permute-done.2.refs_6_
  38.6 2.6 %expert.1 = f32[16,2,128]{2,1,0:T(2,128)S(1)} custom-call(bf16[1024,256]{1,0:T(8,128)(2,1)S(1)} %get-tuple-element.22.refs_0_, bf16[256,2560]{1,0:T(8,128)(2,1)S(1)} %get-tuple-element.25.refs_1_, bf16[256,2560]{1,0:T(8,128)(2,1)S(1)} %get-tuple-element.26.refs_2_, f32[8,1024]{1,0:T(8,128)S(1)} %get-tuple-element.27.refs_3_, ...), custom_call_target="tpu_custom_call" | custom-call | tf_op jit(solution)/shard_map/expert/pallas_call | solution.py:359
  41.1 16.0 %all_to_all.15.parts_ref = f32[16,2,128]{2,1,0:T(2,128)S(1)} all-to-all(f32[16,2,128]{2,1,0:T(2,128)S(1)} %expert.1), channel_id=1, replica_groups=mesh['row'=16,'col'=32] {'row'}, dimensions={0} | all-to-all | bytes 32768 | tf_op jit(solution)/shard_map/all_to_all | solution.py:368
  57.2 15.9 %all_to_all.16.parts_ref = f32[32,8,128]{2,1,0:T(8,128)S(1)} all-to-all(f32[32,8,128]{2,1,0:T(8,128)S(1)} %owner.1), channel_id=1, replica_groups=mesh['row'=16,'col'=32] {'col'}, dimensions={0} | all-to-all | bytes 262144 | tf_op jit(solution)/shard_map/all_to_all | solution.py:377
  73.2 0.6 final.1
  (1 shorter events, 0.0 us)
Async XLA Ops:
  0.6 36.4 %collective-permute-start.1 = (f32[512,1024]{1,0:T(8,128)}, f32[512,1024]{1,0:T(8,128)S(1)}, u32[]{:S(2)}, u32[]{:S(2)}) collective-permute-start(f32[512,1024]{1,0:T(8,128)} %bitcast.1), channel_id=1, source_target_pairs={{0,1},{1,0},{2,3},{3,2},{4,5},{5,4},{6,7},{7,6},{8,9},{9,8},{10,11... | collective-permute-start | bytes 6291464 | tf_op jit(solution)/shard_map/ppermute | solution.py:318
  11.1 22.0 %all-to-all-start = ((f32[16,16,128]{2,1,0:T(8,128)}), f32[16,16,128]{2,1,0:T(8,128)S(1)}, u32[]{:S(2)}, u32[]{:S(2)}) async-start(f32[16,16,128]{2,1,0:T(8,128)} %get-tuple-element.18), calls=%async_computation | async-start | bytes 262144 | tf_op jit(solution)/shard_map/all_to_all | solution.py:316
  20.7 3.2 %collective-permute-start = (f32[40,512]{1,0:T(8,128)S(1)}, f32[40,512]{1,0:T(8,128)S(1)}, u32[]{:S(2)}, u32[]{:S(2)}) collective-permute-start(f32[40,512]{1,0:T(8,128)S(1)} %get-tuple-element.20.refs_1_), channel_id=1, source_target_pairs={{0,1},{1,0},{2,3},{3,2},{4,5},{5,4},{6,7},{7,6},{8,9},{9,8},{10,11... | collective-permute-start | bytes 245768 | tf_op jit(solution)/shard_map/ppermute | solution.py:317
  33.2 5.4 %collective-permute-start.2 = (f32[16,512]{1,0:T(8,128)S(1)}, f32[16,512]{1,0:T(8,128)S(1)}, u32[]{:S(2)}, u32[]{:S(2)}) collective-permute-start(f32[16,512]{1,0:T(8,128)S(1)} %get-tuple-element.31), channel_id=1, source_target_pairs={{0,1},{1,0},{2,3},{3,2},{4,5},{5,4},{6,7},{7,6},{8,9},{9,8},{10,11... | collective-permute-start | bytes 98312 | tf_op jit(solution)/shard_map/ppermute | solution.py:345

commit v4 on v3

--- a/solution.py
+++ b/solution.py
@@ -41,10 +41,9 @@
     peers = member_hbm.shape[0]
     features = points_hbm.shape[1]
     blocks_own, part, _ = tests_ref.shape
-    near = pl.multiple_of(expert // SUBLANES * SUBLANES, SUBLANES)
     mine_at = pl.multiple_of(parity * part, part)
     copies = [
-        pltpu.make_async_copy(member_hbm.at[:, pl.ds(near, SUBLANES), :], member_ref, sems.at[0]),
+        pltpu.make_async_copy(member_hbm.at[:, pl.ds(expert, 1), :], member_ref, sems.at[0]),
         pltpu.make_async_copy(tests_hbm.at[:, pl.ds(mine_at, part), :], tests_ref, sems.at[1]),
         pltpu.make_async_copy(counts_hbm, counts_ref, sems.at[2]),
         pltpu.make_async_copy(points_hbm.at[0], packed_ref.at[0:features], sems.at[3]),
@@ -53,9 +52,7 @@
     for c in copies:
         c.start()
     copies[0].wait()
-    member = member_ref[...].astype(F32)
-    sub = lax.broadcasted_iota(I32, member.shape, 1)
-    mine = jnp.sum(jnp.where(sub == expert - near, member, 0.0), axis=1)
+    mine = jnp.sum(member_ref[...].astype(F32), axis=1)
     row = lax.broadcasted_iota(I32, mine.shape, 0)
     lane = lax.broadcasted_iota(I32, mine.shape, 1)
     wide = [
@@ -304,7 +301,7 @@
         in_specs=[in_hbm] * 5,
         out_specs=(in_hbm,) + (in_vmem,) * 4,
         scratch_shapes=[
-            pltpu.VMEM((rows, SUBLANES, membership.shape[2]), I32),
+            pltpu.VMEM((rows, 1, membership.shape[2]), I32),
             pltpu.VMEM(counts.shape, I32),
             pltpu.VMEM((blocks_own, features // 2, block), F32),
             pltpu.VMEM((rows, features // 2, block), F32),

time: 74.2 us -> 74 us (level)
  no operation moved by 1% of the time
where the time goes in v4:
time: 74 us; the launch traced here: 73.6 us
  blocking collectives  32 us (43%)
  starting transfers between devices  24.4 us (33%)
  Pallas kernels  8.72 us (12%)
  waiting for transfers between devices  7.76 us (10%)
    all_to_all x1, blocking collectives, on_device(): lax.all_to_all(parts, 'row', split_axis=0, concat_axis=0, tiled=True)  16 us
    all_to_all x1, blocking collectives, on_device(): lax.all_to_all(spread, 'col', split_axis=0, concat_axis=0, tiled=True)  15.9 us
    all_to_all x1, starting transfers between devices, on_device(): lax.all_to_all(outgoing, 'row', split_axis=0, concat_axis=0, tiled=True)  9.58 us
    ppermute x1, starting transfers between devices, on_device(): other_factor = lax.ppermute(inverse_factor[0], 'col', swap)  8.75 us
    all_to_all x1, waiting for transfers between devices, on_device(): lax.all_to_all(outgoing, 'row', split_axis=0, concat_axis=0, tiled=True)  6.79 us
    ppermute x1, starting transfers between devices, on_device(): theirs = lax.ppermute(theirs, 'col', swap)  3.88 us
    pallas_call x1, Pallas kernels, on_device(): pl.pallas_call(lambda *refs: expert_kernel(*refs, scale=scale, step=2 * s...  2.55 us
    pallas_call x1, Pallas kernels, on_device(): pl.pallas_call(lambda *refs: points_kernel(*refs, features=features, fact...  2.42 us
  transfers between devices with their start and end apart: 4, of which 2 were waited for; matrix products, arithmetic and copies ran while one was open for 0% of the time, Pallas kernels for 5%

profile of v4, /device:TPU:1, one launch (start us, length us, event | category | flops | bytes accessed | tf_op | source)
XLA Modules:
  0.0 73.6 jit_solution(7014828795886481000)
XLA Ops:
  0.6 8.7 %collective-permute-start.1 = (f32[512,1024]{1,0:T(8,128)}, f32[512,1024]{1,0:T(8,128)S(1)}, u32[]{:S(2)}, u32[]{:S(2)}) collective-permute-start(f32[512,1024]{1,0:T(8,128)} %bitcast.1), channel_id=1, source_target_pairs={{0,1},{1,0},{2,3},{3,2},{4,5},{5,4},{6,7},{7,6},{8,9},{9,8},{10,11... | collective-permute-start | bytes 6291464 | tf_op jit(solution)/shard_map/ppermute | solution.py:315
  9.4 1.6 %send.1 = (f32[16,16,128]{2,1,0:T(8,128)}, f32[40,512]{1,0:T(8,128)S(1)}, f32[4,16,128]{2,1,0:T(8,128)S(1)}, f32[8,16,128]{2,1,0:T(8,128)S(1)}, f32[8,128]{1,0:T(8,128)S(1)}) custom-call(s32[16,16,64]{2,1,0:T(8,128)} %member_hbm.1, s32[1,16]{1,0:T(1,128)} %counts_hbm.1, f32[4,32,128]{2,1,0:T(8,128)} %tests_hbm.1, f32[1,32,512]{2,1,0:T(8,128)} %points_hbm.1, ...), custom_call_target="tpu_custom_call" | custom-call | tf_op jit(solution)/shard_map/send/pallas_call | solution.py:292
  10.9 9.6 %all-to-all-start = ((f32[16,16,128]{2,1,0:T(8,128)}), f32[16,16,128]{2,1,0:T(8,128)S(1)}, u32[]{:S(2)}, u32[]{:S(2)}) async-start(f32[16,16,128]{2,1,0:T(8,128)} %get-tuple-element.18), calls=%async_computation | async-start | bytes 262144 | tf_op jit(solution)/shard_map/all_to_all | solution.py:313
  20.5 2.2 %collective-permute-start = (f32[40,512]{1,0:T(8,128)S(1)}, f32[40,512]{1,0:T(8,128)S(1)}, u32[]{:S(2)}, u32[]{:S(2)}) collective-permute-start(f32[40,512]{1,0:T(8,128)S(1)} %get-tuple-element.20.refs_1_), channel_id=1, source_target_pairs={{0,1},{1,0},{2,3},{3,2},{4,5},{5,4},{6,7},{7,6},{8,9},{9,8},{10,11... | collective-permute-start | bytes 245768 | tf_op jit(solution)/shard_map/ppermute | solution.py:314
  22.7 1.0 %collective-permute-done.refs_2_ = f32[40,512]{1,0:T(8,128)S(1)} collective-permute-done((f32[40,512]{1,0:T(8,128)S(1)}, f32[40,512]{1,0:T(8,128)S(1)}, u32[]{:S(2)}, u32[]{:S(2)}) %collective-permute-start) | collective-permute-done | bytes 81952 | tf_op jit(solution)/shard_map/ppermute | solution.py:314
  23.7 2.4 %points.1 = (bf16[1024,256]{1,0:T(8,128)(2,1)S(1)}, bf16[1024,128]{1,0:T(8,128)(2,1)S(1)}, f32[8,1024]{1,0:T(8,128)S(1)}) custom-call(f32[8,128]{1,0:T(8,128)S(1)} %get-tuple-element.19.refs_0_, f32[40,512]{1,0:T(8,128)S(1)} %get-tuple-element.20.refs_1_, f32[40,512]{1,0:T(8,128)S(1)} %collective-permute-done.refs_2_, f32[1,512,1024]{2,1,0:T(8,128)} %refs_0_.1), custom_call_target="tpu_custom_call" | custom-call | tf_op jit(solution)/shard_map/points/pallas_call | solution.py:320
  26.1 6.8 %all-to-all-done.tests_ref = f32[16,16,128]{2,1,0:T(8,128)S(1)} async-done(((f32[16,16,128]{2,1,0:T(8,128)}), f32[16,16,128]{2,1,0:T(8,128)S(1)}, u32[]{:S(2)}, u32[]{:S(2)}) %all-to-all-start) | async-done | bytes 131104 | tf_op jit(solution)/shard_map/all_to_all | solution.py:313
  32.9 0.1 pick.1
  33.0 3.9 %collective-permute-start.2 = (f32[16,512]{1,0:T(8,128)S(1)}, f32[16,512]{1,0:T(8,128)S(1)}, u32[]{:S(2)}, u32[]{:S(2)}) collective-permute-start(f32[16,512]{1,0:T(8,128)S(1)} %get-tuple-element.31), channel_id=1, source_target_pairs={{0,1},{1,0},{2,3},{3,2},{4,5},{5,4},{6,7},{7,6},{8,9},{9,8},{10,11... | collective-permute-start | bytes 98312 | tf_op jit(solution)/shard_map/ppermute | solution.py:342
  36.9 0.0 collective-permute-done.1.refs_1_
  36.9 1.5 %factor.1 = (bf16[256,2560]{1,0:T(8,128)(2,1)S(1)}, bf16[256,2560]{1,0:T(8,128)(2,1)S(1)}, f32[8,1024]{1,0:T(8,128)S(1)}) custom-call(f32[1,512,1024]{2,1,0:T(8,128)} %refs_0_.1, f32[512,1024]{1,0:T(8,128)S(1)} %collective-permute-done.1.refs_1_, bf16[1024,128]{1,0:T(8,128)(2,1)S(1)} %get-tuple-element.23.refs_2_, f32[8,1024]{1,0:T(8,128)S(1)} %get-tuple-element.24.refs_3_), custom_call_target="tpu_custom_call" | custom-call | tf_op jit(solution)/shard_map/factor/pallas_call | solution.py:343
  38.4 0.0 collective-permute-done.2.refs_6_
  38.4 2.6 %expert.1 = f32[16,2,128]{2,1,0:T(2,128)S(1)} custom-call(bf16[1024,256]{1,0:T(8,128)(2,1)S(1)} %get-tuple-element.22.refs_0_, bf16[256,2560]{1,0:T(8,128)(2,1)S(1)} %get-tuple-element.25.refs_1_, bf16[256,2560]{1,0:T(8,128)(2,1)S(1)} %get-tuple-element.26.refs_2_, f32[8,1024]{1,0:T(8,128)S(1)} %get-tuple-element.27.refs_3_, ...), custom_call_target="tpu_custom_call" | custom-call | tf_op jit(solution)/shard_map/expert/pallas_call | solution.py:356
  41.0 16.0 %all_to_all.15.parts_ref = f32[16,2,128]{2,1,0:T(2,128)S(1)} all-to-all(f32[16,2,128]{2,1,0:T(2,128)S(1)} %expert.1), channel_id=1, replica_groups=mesh['row'=16,'col'=32] {'row'}, dimensions={0} | all-to-all | bytes 32768 | tf_op jit(solution)/shard_map/all_to_all | solution.py:365
  57.1 15.9 %all_to_all.16.parts_ref = f32[32,8,128]{2,1,0:T(8,128)S(1)} all-to-all(f32[32,8,128]{2,1,0:T(8,128)S(1)} %owner.1), channel_id=1, replica_groups=mesh['row'=16,'col'=32] {'col'}, dimensions={0} | all-to-all | bytes 262144 | tf_op jit(solution)/shard_map/all_to_all | solution.py:374
  73.0 0.6 final.1
  (1 shorter events, 0.0 us)
Async XLA Ops:
  0.6 36.3 %collective-permute-start.1 = (f32[512,1024]{1,0:T(8,128)}, f32[512,1024]{1,0:T(8,128)S(1)}, u32[]{:S(2)}, u32[]{:S(2)}) collective-permute-start(f32[512,1024]{1,0:T(8,128)} %bitcast.1), channel_id=1, source_target_pairs={{0,1},{1,0},{2,3},{3,2},{4,5},{5,4},{6,7},{7,6},{8,9},{9,8},{10,11... | collective-permute-start | bytes 6291464 | tf_op jit(solution)/shard_map/ppermute | solution.py:315
  10.9 22.0 %all-to-all-start = ((f32[16,16,128]{2,1,0:T(8,128)}), f32[16,16,128]{2,1,0:T(8,128)S(1)}, u32[]{:S(2)}, u32[]{:S(2)}) async-start(f32[16,16,128]{2,1,0:T(8,128)} %get-tuple-element.18), calls=%async_computation | async-start | bytes 262144 | tf_op jit(solution)/shard_map/all_to_all | solution.py:313
  20.5 3.2 %collective-permute-start = (f32[40,512]{1,0:T(8,128)S(1)}, f32[40,512]{1,0:T(8,128)S(1)}, u32[]{:S(2)}, u32[]{:S(2)}) collective-permute-start(f32[40,512]{1,0:T(8,128)S(1)} %get-tuple-element.20.refs_1_), channel_id=1, source_target_pairs={{0,1},{1,0},{2,3},{3,2},{4,5},{5,4},{6,7},{7,6},{8,9},{9,8},{10,11... | collective-permute-start | bytes 245768 | tf_op jit(solution)/shard_map/ppermute | solution.py:314
  33.0 5.4 %collective-permute-start.2 = (f32[16,512]{1,0:T(8,128)S(1)}, f32[16,512]{1,0:T(8,128)S(1)}, u32[]{:S(2)}, u32[]{:S(2)}) collective-permute-start(f32[16,512]{1,0:T(8,128)S(1)} %get-tuple-element.31), channel_id=1, source_target_pairs={{0,1},{1,0},{2,3},{3,2},{4,5},{5,4},{6,7},{7,6},{8,9},{9,8},{10,11... | collective-permute-start | bytes 98312 | tf_op jit(solution)/shard_map/ppermute | solution.py:342

commit v5 on v3

--- a/solution.py
+++ b/solution.py
@@ -133,7 +133,7 @@
     _, _, parity = place()
     half = own_ref.shape[1]
     coming = factor_copies(f_hbm, f_ref, sems, step)
-    for c in coming:
+    for c in coming[::-1]:
         c.start()
     valid = valid_ref[0:1, 0:1]
 
@@ -166,7 +166,7 @@
     lane = lax.broadcasted_iota(I32, y.shape, 1)
     y_ref[...] = jnp.where(lane < LANES // 2, yh, y - yh).astype(BF16)
     sums = [jnp.zeros((SUBLANES, LANES), F32) for _ in range(2 * half // LANES)]
-    for a, c in enumerate(coming):
+    for a, c in reversed(list(enumerate(coming))):
         c.wait()
         f = factor_block(f_ref, a, step)
         add_alpha(sums, f, two_parts(f), y_ref)
@@ -176,12 +176,12 @@
 
 def factor_kernel(own_f_hbm, other_f_ref, y_ref, own_alpha_ref, fh_ref, fl_ref, alpha_ref, own_f_ref, sems, *, step):
     coming = factor_copies(own_f_hbm, own_f_ref, sems, step)
-    for c in coming:
+    for c in coming[::-1]:
         c.start()
     sums = [own_alpha_ref[:, c : c + LANES] for c in range(0, y_ref.shape[0], LANES)]
     for which, f_ref in ((1, other_f_ref), (0, own_f_ref)):
         rows = slice(step * which, step * which + step)
-        for a, c in enumerate(coming):
+        for a, c in reversed(list(enumerate(coming))):
             if which == 0:
                 c.wait()
             f = factor_block(f_ref, a, step)

time: 74.2 us -> 74.1 us (level)
  no operation moved by 1% of the time
where the time goes in v5:
time: 74.1 us; the launch traced here: 73.7 us
  blocking collectives  32 us (43%)
  starting transfers between devices  24.4 us (33%)
  Pallas kernels  8.73 us (12%)
  waiting for transfers between devices  7.86 us (11%)
    all_to_all x1, blocking collectives, on_device(): lax.all_to_all(parts, 'row', split_axis=0, concat_axis=0, tiled=True)  16 us
    all_to_all x1, blocking collectives, on_device(): lax.all_to_all(spread, 'col', split_axis=0, concat_axis=0, tiled=True)  15.9 us
    all_to_all x1, starting transfers between devices, on_device(): lax.all_to_all(outgoing, 'row', split_axis=0, concat_axis=0, tiled=True)  9.58 us
    ppermute x1, starting transfers between devices, on_device(): other_factor = lax.ppermute(inverse_factor[0], 'col', swap)  8.75 us
    all_to_all x1, waiting for transfers between devices, on_device(): lax.all_to_all(outgoing, 'row', split_axis=0, concat_axis=0, tiled=True)  6.89 us
    ppermute x1, starting transfers between devices, on_device(): theirs = lax.ppermute(theirs, 'col', swap)  3.88 us
    pallas_call x1, Pallas kernels, on_device(): pl.pallas_call(lambda *refs: expert_kernel(*refs, scale=scale, step=2 * s...  2.56 us
    pallas_call x1, Pallas kernels, on_device(): pl.pallas_call(lambda *refs: points_kernel(*refs, features=features, fact...  2.32 us
  transfers between devices with their start and end apart: 4, of which 2 were waited for; matrix products, arithmetic and copies ran while one was open for 0% of the time, Pallas kernels for 5%

profile of v5, /device:TPU:1, one launch (start us, length us, event | category | flops | bytes accessed | tf_op | source)
XLA Modules:
  0.0 73.7 jit_solution(5533482504541479946)
XLA Ops:
  0.6 8.7 %collective-permute-start.1 = (f32[512,1024]{1,0:T(8,128)}, f32[512,1024]{1,0:T(8,128)S(1)}, u32[]{:S(2)}, u32[]{:S(2)}) collective-permute-start(f32[512,1024]{1,0:T(8,128)} %bitcast.1), channel_id=1, source_target_pairs={{0,1},{1,0},{2,3},{3,2},{4,5},{5,4},{6,7},{7,6},{8,9},{9,8},{10,11... | collective-permute-start | bytes 6291464 | tf_op jit(solution)/shard_map/ppermute | solution.py:318
  9.4 1.7 %send.1 = (f32[16,16,128]{2,1,0:T(8,128)}, f32[40,512]{1,0:T(8,128)S(1)}, f32[4,16,128]{2,1,0:T(8,128)S(1)}, f32[8,16,128]{2,1,0:T(8,128)S(1)}, f32[8,128]{1,0:T(8,128)S(1)}) custom-call(s32[16,16,64]{2,1,0:T(8,128)} %member_hbm.1, s32[1,16]{1,0:T(1,128)} %counts_hbm.1, f32[4,32,128]{2,1,0:T(8,128)} %tests_hbm.1, f32[1,32,512]{2,1,0:T(8,128)} %points_hbm.1, ...), custom_call_target="tpu_custom_call" | custom-call | tf_op jit(solution)/shard_map/send/pallas_call | solution.py:295
  11.1 9.6 %all-to-all-start = ((f32[16,16,128]{2,1,0:T(8,128)}), f32[16,16,128]{2,1,0:T(8,128)S(1)}, u32[]{:S(2)}, u32[]{:S(2)}) async-start(f32[16,16,128]{2,1,0:T(8,128)} %get-tuple-element.18), calls=%async_computation | async-start | bytes 262144 | tf_op jit(solution)/shard_map/all_to_all | solution.py:316
  20.7 2.2 %collective-permute-start = (f32[40,512]{1,0:T(8,128)S(1)}, f32[40,512]{1,0:T(8,128)S(1)}, u32[]{:S(2)}, u32[]{:S(2)}) collective-permute-start(f32[40,512]{1,0:T(8,128)S(1)} %get-tuple-element.20.refs_1_), channel_id=1, source_target_pairs={{0,1},{1,0},{2,3},{3,2},{4,5},{5,4},{6,7},{7,6},{8,9},{9,8},{10,11... | collective-permute-start | bytes 245768 | tf_op jit(solution)/shard_map/ppermute | solution.py:317
  22.9 1.0 %collective-permute-done.refs_2_ = f32[40,512]{1,0:T(8,128)S(1)} collective-permute-done((f32[40,512]{1,0:T(8,128)S(1)}, f32[40,512]{1,0:T(8,128)S(1)}, u32[]{:S(2)}, u32[]{:S(2)}) %collective-permute-start) | collective-permute-done | bytes 81952 | tf_op jit(solution)/shard_map/ppermute | solution.py:317
  23.9 2.3 %points.1 = (bf16[1024,256]{1,0:T(8,128)(2,1)S(1)}, bf16[1024,128]{1,0:T(8,128)(2,1)S(1)}, f32[8,1024]{1,0:T(8,128)S(1)}) custom-call(f32[8,128]{1,0:T(8,128)S(1)} %get-tuple-element.19.refs_0_, f32[40,512]{1,0:T(8,128)S(1)} %get-tuple-element.20.refs_1_, f32[40,512]{1,0:T(8,128)S(1)} %collective-permute-done.refs_2_, f32[1,512,1024]{2,1,0:T(8,128)} %refs_0_.1), custom_call_target="tpu_custom_call" | custom-call | tf_op jit(solution)/shard_map/points/pallas_call | solution.py:323
  26.2 6.9 %all-to-all-done.tests_ref = f32[16,16,128]{2,1,0:T(8,128)S(1)} async-done(((f32[16,16,128]{2,1,0:T(8,128)}), f32[16,16,128]{2,1,0:T(8,128)S(1)}, u32[]{:S(2)}, u32[]{:S(2)}) %all-to-all-start) | async-done | bytes 131104 | tf_op jit(solution)/shard_map/all_to_all | solution.py:316
  33.1 0.1 pick.1
  33.2 3.9 %collective-permute-start.2 = (f32[16,512]{1,0:T(8,128)S(1)}, f32[16,512]{1,0:T(8,128)S(1)}, u32[]{:S(2)}, u32[]{:S(2)}) collective-permute-start(f32[16,512]{1,0:T(8,128)S(1)} %get-tuple-element.31), channel_id=1, source_target_pairs={{0,1},{1,0},{2,3},{3,2},{4,5},{5,4},{6,7},{7,6},{8,9},{9,8},{10,11... | collective-permute-start | bytes 98312 | tf_op jit(solution)/shard_map/ppermute | solution.py:345
  37.1 0.0 collective-permute-done.1.refs_1_
  37.1 1.4 %factor.1 = (bf16[256,2560]{1,0:T(8,128)(2,1)S(1)}, bf16[256,2560]{1,0:T(8,128)(2,1)S(1)}, f32[8,1024]{1,0:T(8,128)S(1)}) custom-call(f32[1,512,1024]{2,1,0:T(8,128)} %refs_0_.1, f32[512,1024]{1,0:T(8,128)S(1)} %collective-permute-done.1.refs_1_, bf16[1024,128]{1,0:T(8,128)(2,1)S(1)} %get-tuple-element.23.refs_2_, f32[8,1024]{1,0:T(8,128)S(1)} %get-tuple-element.24.refs_3_), custom_call_target="tpu_custom_call" | custom-call | tf_op jit(solution)/shard_map/factor/pallas_call | solution.py:346
  38.5 0.0 collective-permute-done.2.refs_6_
  38.5 2.6 %expert.1 = f32[16,2,128]{2,1,0:T(2,128)S(1)} custom-call(bf16[1024,256]{1,0:T(8,128)(2,1)S(1)} %get-tuple-element.22.refs_0_, bf16[256,2560]{1,0:T(8,128)(2,1)S(1)} %get-tuple-element.25.refs_1_, bf16[256,2560]{1,0:T(8,128)(2,1)S(1)} %get-tuple-element.26.refs_2_, f32[8,1024]{1,0:T(8,128)S(1)} %get-tuple-element.27.refs_3_, ...), custom_call_target="tpu_custom_call" | custom-call | tf_op jit(solution)/shard_map/expert/pallas_call | solution.py:359
  41.1 16.0 %all_to_all.15.parts_ref = f32[16,2,128]{2,1,0:T(2,128)S(1)} all-to-all(f32[16,2,128]{2,1,0:T(2,128)S(1)} %expert.1), channel_id=1, replica_groups=mesh['row'=16,'col'=32] {'row'}, dimensions={0} | all-to-all | bytes 32768 | tf_op jit(solution)/shard_map/all_to_all | solution.py:368
  57.2 15.9 %all_to_all.16.parts_ref = f32[32,8,128]{2,1,0:T(8,128)S(1)} all-to-all(f32[32,8,128]{2,1,0:T(8,128)S(1)} %owner.1), channel_id=1, replica_groups=mesh['row'=16,'col'=32] {'col'}, dimensions={0} | all-to-all | bytes 262144 | tf_op jit(solution)/shard_map/all_to_all | solution.py:377
  73.1 0.6 final.1
  (1 shorter events, 0.0 us)
Async XLA Ops:
  0.6 36.4 %collective-permute-start.1 = (f32[512,1024]{1,0:T(8,128)}, f32[512,1024]{1,0:T(8,128)S(1)}, u32[]{:S(2)}, u32[]{:S(2)}) collective-permute-start(f32[512,1024]{1,0:T(8,128)} %bitcast.1), channel_id=1, source_target_pairs={{0,1},{1,0},{2,3},{3,2},{4,5},{5,4},{6,7},{7,6},{8,9},{9,8},{10,11... | collective-permute-start | bytes 6291464 | tf_op jit(solution)/shard_map/ppermute | solution.py:318
  11.1 22.0 %all-to-all-start = ((f32[16,16,128]{2,1,0:T(8,128)}), f32[16,16,128]{2,1,0:T(8,128)S(1)}, u32[]{:S(2)}, u32[]{:S(2)}) async-start(f32[16,16,128]{2,1,0:T(8,128)} %get-tuple-element.18), calls=%async_computation | async-start | bytes 262144 | tf_op jit(solution)/shard_map/all_to_all | solution.py:316
  20.7 3.2 %collective-permute-start = (f32[40,512]{1,0:T(8,128)S(1)}, f32[40,512]{1,0:T(8,128)S(1)}, u32[]{:S(2)}, u32[]{:S(2)}) collective-permute-start(f32[40,512]{1,0:T(8,128)S(1)} %get-tuple-element.20.refs_1_), channel_id=1, source_target_pairs={{0,1},{1,0},{2,3},{3,2},{4,5},{5,4},{6,7},{7,6},{8,9},{9,8},{10,11... | collective-permute-start | bytes 245768 | tf_op jit(solution)/shard_map/ppermute | solution.py:317
  33.2 5.3 %collective-permute-start.2 = (f32[16,512]{1,0:T(8,128)S(1)}, f32[16,512]{1,0:T(8,128)S(1)}, u32[]{:S(2)}, u32[]{:S(2)}) collective-permute-start(f32[16,512]{1,0:T(8,128)S(1)} %get-tuple-element.31), channel_id=1, source_target_pairs={{0,1},{1,0},{2,3},{3,2},{4,5},{5,4},{6,7},{7,6},{8,9},{9,8},{10,11... | collective-permute-start | bytes 98312 | tf_op jit(solution)/shard_map/ppermute | solution.py:345
